TPU v7x, 16 devices: a 4x2x1 block of a 4x4x8 slice. The times are simulated.
16 devices in a mesh: dp: 2 (over y, z), tp: 8 (over x, core).
Axes of the slice: x: 4, y: 2, z: 1, core: 2. Of those that a mesh axis runs over, the one named last changes fastest.
The devices are a block of a 4x4x8 slice.
Arguments:
- x_rows: bfloat16 [16384, 2304], P(('dp', 'tp')), parts along dimension 0
- norm_gain: float32 [2304], replicated
- w_q: bfloat16 [2304, 8, 256], P(None, 'tp')
- w_k: bfloat16 [2304, 1024], P(None, 'tp')
- w_v: bfloat16 [2304, 1024], P(None, 'tp')
Outputs:
- output 1: bfloat16 [16384, 8, 256], P('dp', 'tp'), parts along dimension 0
- output 2: bfloat16 [16384, 8, 256], P('dp', 'tp'), parts along dimension 0
- output 3: bfloat16 [16384, 8, 256], P('dp', 'tp'), parts along dimension 0
There are 2 independent parts. A program takes and returns all parts, laid end to end along the dimension named above; an argument that names none is the same for every part.
All inputs are finite; a program needn't handle non-finite values.
Results may differ from a plain program's by a relative error of at most 0.001.
Values are sent between devices in bfloat16 or wider.
A program may use at most 768 MiB of HBM per device.

v0:
```python
import jax
import jax.numpy as jnp
from jax import lax
from jax.sharding import PartitionSpec as P

EPSILON = 1e-6


def solution(mesh):
    group_size = mesh.shape["tp"]

    def head_pieces(piece, head_share):
        member = lax.axis_index("tp") % head_share
        received = [piece]
        for step_ahead in range(1, head_share):
            send_pairs = [(source, (source // head_share) * head_share + (source % head_share - step_ahead) % head_share) for source in range(group_size)]
            received.append(lax.ppermute(piece, "tp", send_pairs))
        joined = jnp.concatenate(received, axis=1)
        return jnp.roll(joined, member * piece.shape[1], axis=1)

    def local_step(x_rows, norm_gain, w_q, w_k, w_v):
        x_wide = x_rows.astype(jnp.float32)
        mean_sq = jnp.mean(x_wide * x_wide, axis=-1, keepdims=True)
        normed = (x_wide * lax.rsqrt(mean_sq + EPSILON) * norm_gain).astype(jnp.bfloat16)
        gathered = lax.all_gather(normed, "tp", axis=0, tiled=True)
        q_local = jnp.einsum("td,dhe->the", gathered, w_q, preferred_element_type=jnp.float32).astype(jnp.bfloat16)
        k_piece = jnp.dot(gathered, w_k, preferred_element_type=jnp.float32).astype(jnp.bfloat16)
        v_piece = jnp.dot(gathered, w_v, preferred_element_type=jnp.float32).astype(jnp.bfloat16)
        head_share = w_q.shape[2] // w_k.shape[1]
        k_head = head_pieces(k_piece, head_share)
        v_head = head_pieces(v_piece, head_share)
        return q_local, k_head[:, None, :], v_head[:, None, :]

    return jax.shard_map(local_step, mesh=mesh, in_specs=(P(("dp", "tp"), None), P(None), P(None, "tp", None), P(None, "tp"), P(None, "tp")), out_specs=(P("dp", "tp", None), P("dp", "tp", None), P("dp", "tp", None)), check_vma=False)
```

profile of v0, /device:TPU:113, one launch (start us, length us, event | category | flops | bytes accessed | tf_op | source)
XLA Modules:
  0.0 283.8 jit_solution(13665885749203106625)
XLA Ops:
  7.2 0.0 copy-start
  7.2 0.0 copy-start.1
  7.2 0.1 all-gather.2.cloned.1.call-start
  7.3 3.5 %fusion.1 = f32[1024]{0:T(1024)S(1)} fusion(bf16[1024,2304]{1,0:T(8,128)(2,1)} %param.7), kind=kLoop, calls=%fused_computation.6 | loop fusion | flops 7076864 | bytes 4722688 | tf_op jit(solution)/shard_map/reduce_sum | solution.py:23
  10.7 5.6 %fusion.3 = bf16[1024,2304]{1,0:T(8,128)(2,1)} fusion(bf16[1024,2304]{1,0:T(8,128)(2,1)} %param.7, f32[2304]{0:T(1024)} %param.8, f32[1024]{0:T(1024)S(1)} %add_rsqrt_fusion), kind=kLoop, calls=%fused_computation.8 | loop fusion | flops 9437184 | bytes 9450496 | tf_op jit(solution)/shard_map/convert_element_type | solution.py:24
  16.4 0.1 all-gather.2.cloned.1.call-update
  16.5 175.4 %all-gather.2.cloned.1.call-done = bf16[8192,2304]{1,0:T(8,128)(2,1)} async-done(((bf16[1024,2304]{1,0:T(8,128)(2,1)}), bf16[8192,2304]{1,0:T(8,128)(2,1)}) %all-gather.2.cloned.1.call-update) | async-done | bytes 37748752 | tf_op jit(solution)/shard_map/all_gather | solution.py:25
  191.9 0.0 copy-done.1
  191.9 19.2 %convolution_convert_fusion.2 = bf16[8192,128]{0,1:T(8,128)(2,1)} fusion(bf16[8192,2304]{1,0:T(8,128)(2,1)} %all-gather.2.cloned.1.call-done, bf16[2304,128]{1,0:T(8,128)(2,1)S(1)} %copy-done.1), kind=kOutput, calls=%fused_computation.5 | convolution fusion | flops 4832886784 | bytes 40435712 | tf_op jit(solution)/shard_map/dot_general | solution.py:27
  211.1 0.3 collective-permute-start
  211.4 17.9 %convolution_convert_fusion.1 = bf16[8192,128]{0,1:T(8,128)(2,1)S(1)} fusion(bf16[8192,2304]{1,0:T(8,128)(2,1)} %all-gather.2.cloned.1.call-done, bf16[2304,128]{1,0:T(8,128)(2,1)} %param.11), kind=kOutput, calls=%fused_computation.4 | convolution fusion | flops 4832886784 | bytes 40435712 | tf_op jit(solution)/shard_map/dot_general | solution.py:28
  229.3 0.3 collective-permute-start.1
  229.6 0.0 copy-done
  229.6 18.6 %fusion = bf16[8192,1,256]{2,0,1:T(8,128)(2,1)} fusion(bf16[8192,2304]{1,0:T(8,128)(2,1)} %all-gather.2.cloned.1.call-done, bf16[2304,1,256]{2,0,1:T(8,128)(2,1)S(1)} %copy-done), kind=kOutput, calls=%fused_computation.3 | convolution fusion | flops 9665773568 | bytes 43122688 | tf_op jit(solution)/shard_map/td,dhe->the/dot_general | solution.py:26
  248.3 0.0 collective-permute-done
  248.3 8.1 %fusion.8 = bf16[8192,256]{0,1:T(8,128)(2,1)} fusion(s32[]{:T(128)S(6)} %select_n.22, bf16[8192,128]{0,1:T(8,128)(2,1)} %convolution_convert_fusion.2, bf16[8192,128]{0,1:T(8,128)(2,1)} %collective-permute-done), kind=kLoop, calls=%fused_computation.21 | loop fusion | flops 16777216 | bytes 8388612 | tf_op jit(solution)/shard_map/jit(_roll_dynamic)/concatenate | solution.py:19
  256.3 6.4 %copy.8 = bf16[8192,256]{1,0:T(8,128)(2,1)} copy(bf16[8192,256]{0,1:T(8,128)(2,1)} %fusion.8) | data formatting | bytes 8388608 | tf_op jit(solution)/shard_map/jit(_roll_dynamic)/dynamic_slice | solution.py:19
  262.7 0.0 collective-permute-done.1
  262.7 7.9 %fusion.5 = bf16[8192,256]{0,1:T(8,128)(2,1)} fusion(s32[]{:T(128)S(6)} %select_n.22, bf16[8192,128]{0,1:T(8,128)(2,1)S(1)} %convolution_convert_fusion.1, bf16[8192,128]{0,1:T(8,128)(2,1)} %collective-permute-done.1), kind=kLoop, calls=%fused_computation.18 | loop fusion | flops 16777216 | bytes 8388612 | tf_op jit(solution)/shard_map/jit(_roll_dynamic)/concatenate | solution.py:19
  270.6 6.4 %copy.9 = bf16[8192,256]{1,0:T(8,128)(2,1)} copy(bf16[8192,256]{0,1:T(8,128)(2,1)} %fusion.5) | data formatting | bytes 8388608 | tf_op jit(solution)/shard_map/jit(_roll_dynamic)/dynamic_slice | solution.py:19
  (1 shorter events, 0.0 us)
Async XLA Ops:
  7.2 222.5 %copy-start = (bf16[2304,1,256]{2,0,1:T(8,128)(2,1)S(1)}, bf16[2304,1,256]{2,0,1:T(8,128)(2,1)}, u32[]{:S(2)}) copy-start(bf16[2304,1,256]{2,0,1:T(8,128)(2,1)} %param.9) | copy-start | bytes 3538948
  7.2 184.7 %copy-start.1 = (bf16[2304,128]{1,0:T(8,128)(2,1)S(1)}, bf16[2304,128]{1,0:T(8,128)(2,1)}, u32[]{:S(2)}) copy-start(bf16[2304,128]{1,0:T(8,128)(2,1)} %param.10) | copy-start | bytes 1769476
  7.2 184.7 %all-gather.2.cloned.1.call-start = ((), (), s32[]{:S(2)}) async-start(), calls=%async_computation | async-start | bytes 42467328 | tf_op jit(solution)/shard_map/all_gather | solution.py:25
  211.1 37.1 %collective-permute-start = (bf16[8192,128]{0,1:T(8,128)(2,1)}, bf16[8192,128]{0,1:T(8,128)(2,1)}, u32[]{:S(2)}, u32[]{:S(2)}) collective-permute-start(bf16[8192,128]{0,1:T(8,128)(2,1)} %convolution_convert_fusion.2), channel_id=1, source_target_pairs={{0,1},{1,0},{2,3},{3,2},{4,5},{5,4},{6,7},{7,6},{8,9},{9,8},{10,11... | collective-permute-start | bytes 6291464 | tf_op jit(solution)/shard_map/ppermute | solution.py:17
  229.3 33.4 %collective-permute-start.1 = (bf16[8192,128]{0,1:T(8,128)(2,1)S(1)}, bf16[8192,128]{0,1:T(8,128)(2,1)}, u32[]{:S(2)}, u32[]{:S(2)}) collective-permute-start(bf16[8192,128]{0,1:T(8,128)(2,1)S(1)} %convolution_convert_fusion.1), channel_id=1, source_target_pairs={{0,1},{1,0},{2,3},{3,2},{4,5},{5,4},{6,7},{7,6},{8,9},{9,8},{10,11... | collective-permute-start | bytes 6291464 | tf_op jit(solution)/shard_map/ppermute | solution.py:17
Sparse Core Ops, SparseCore 0:
  16.6 175.2 all-gather.1
where the time goes:
time: 284 us
  waiting for transfers between devices  175 us (62%)
  matrix products  55.8 us (20%)
  other arithmetic  25 us (9%)
  between operations  14.1 us (5%)
  local copies, waits for them, and re-layouts  12.7 us (4%)
    all_gather x1, waiting for transfers between devices, local_step(): gathered = lax.all_gather(normed, 'tp', axis=0, tiled=True)  175 us
    dot_general x1, matrix products, local_step(): jnp.dot(gathered, w_k, preferred_element_type=jnp.float32)  19.2 us
    dot_general x1, matrix products, local_step(): jnp.einsum('td,dhe->the', gathered, w_q, preferred_element_type=jnp.float32)  18.6 us
    dot_general x1, matrix products, local_step(): jnp.dot(gathered, w_v, preferred_element_type=jnp.float32)  17.9 us
    concatenate x2, other arithmetic, head_pieces(): return jnp.roll(joined, member * piece.shape[1], axis=1)  15.9 us
    dynamic_slice x2, local copies, waits for them, and re-layouts, head_pieces(): return jnp.roll(joined, member * piece.shape[1], axis=1)  12.7 us
  transfers between devices with their start and end apart: 3, of which 1 were waited for; matrix products, arithmetic and copies ran while one was open for 18% of the time, Pallas kernels for 0%

commit v1 on v0

v1 whole, which is shorter than its diff:
```python
import functools

import jax
import jax.numpy as jnp
from jax import lax
from jax.experimental import pallas as pl
from jax.experimental.pallas import tpu as pltpu
from jax.sharding import PartitionSpec as P

EPSILON = 1e-6
LANES = 128
NORM_ROWS = 32
CHUNK = 128
OWN_ROWS = 256
MESH = pl.DeviceIdType.MESH


def exchange(chips, x, gain, wq, wk, wv, oq, okv, n, w, slq, srq, srkv, x_sem, wl_sem, wl_s, wl_r, wx_s, wx_r, wg_s, wg_r, wd_s, wd_r, n_s, n_r,
             oq_s, oq_r, okv_s, okv_r, rq_s, rq_r, rkv_s, rkv_r, lq_s, lq_r, lkv_s, lkv_r, fk_s, fk_r):
    rows, depth = x.shape
    chunks = rows // CHUNK
    group = lax.axis_index("dp")
    device = lax.axis_index("tp")
    half = lax.rem(group, 2)
    core = lax.rem(device, 2)
    chip = lax.div(device, 2)
    token_chip = chip + 1 - 2 * lax.rem(chip, 2)
    weight_chip = chips - 1 - chip
    far_chip = weight_chip + 1 - 2 * lax.rem(weight_chip, 2)
    other_core = 1 - core
    partner = {"tp": 2 * chip + other_core}
    token_peer = {"tp": 2 * token_chip + core}
    weight_peer = {"tp": 2 * weight_chip + core}
    group_peer = {"dp": group + 1 - 2 * half}

    def weight_core(c):
        return {"tp": 2 * weight_chip + c}

    def remote(src, dst, send, recv, to):
        return pltpu.make_async_remote_copy(src_ref=src, dst_ref=dst, send_sem=send, recv_sem=recv, device_id=to, device_id_type=MESH)

    def block(c, on_chip):
        return pl.multiple_of((2 * on_chip + c) * rows, rows)

    def chunk_of(j):
        return pl.ds(pl.multiple_of(j * CHUNK, CHUNK), CHUNK)

    def load_x(j):
        return pltpu.make_async_copy(x.at[chunk_of(j)], n.at[0, chunk_of(j)], x_sem.at[j])

    for j in range(chunks):
        load_x(j).start()

    q_half = [wq.at[:, pl.ds(h * LANES, LANES)] for h in range(2)]
    kv = [wk, wv]

    barrier = pltpu.get_barrier_semaphore()
    for peer in (partner, token_peer, weight_peer, weight_core(other_core), group_peer):
        pl.semaphore_signal(barrier, inc=1, device_id=peer, device_id_type=MESH)
    pl.semaphore_wait(barrier, 5)

    w_first = w.at[1, half, core, :, pl.ds(0, LANES)]
    w_second = w.at[1, half, core, :, pl.ds(LANES, LANES)]
    remote(wq.at[:, pl.ds(pl.multiple_of(half * LANES, LANES), LANES)], w_first, wx_s, wx_r.at[0], weight_peer).start()
    for h in range(2):
        @pl.when(half == h)
        def _():
            remote(kv[h], w_second, wx_s, wx_r.at[1], weight_peer).start()
    for h in range(2):
        for part, src in enumerate((q_half[h], kv[h])):
            dst = w.at[0, h, core, :, pl.ds(part * LANES, LANES)]
            remote(src, dst, wl_s, wl_r, partner).start()
            pltpu.make_async_copy(src, dst, wl_sem).start()

    def send_n(j):
        return remote(n.at[0, chunk_of(j)], n.at[1, chunk_of(j)], n_s, n_r.at[j], token_peer)

    @pl.loop(0, chunks)
    def _(j):
        load_x(j).wait()

        @pl.loop(0, CHUNK // NORM_ROWS)
        def _(i):
            at = pl.ds(pl.multiple_of(j * CHUNK + i * NORM_ROWS, NORM_ROWS), NORM_ROWS)
            wide = n[0, at, :].astype(jnp.float32)
            mean_sq = jnp.mean(wide * wide, axis=-1, keepdims=True)
            n[0, at, :] = (wide * lax.rsqrt(mean_sq + EPSILON) * gain[...]).astype(jnp.bfloat16)

        send_n(j).start()

    def product(blk, at, side, h, c):
        return jnp.dot(n[blk, at, :], w[side, h, c], preferred_element_type=jnp.float32).astype(jnp.bfloat16)

    def local_products(blk, base, start, size):
        at = pl.ds(start, size)
        out = pl.ds(pl.multiple_of(base + start, size), size)

        @pl.loop(0, 2)
        def _(h):
            for b in range(2):
                c = lax.rem(core + b, 2)
                both = product(blk, at, 0, h, c)
                if b == 0:
                    oq[h, out, :] = both[:, :LANES]
                else:
                    slq[blk, h, at, :] = both[:, :LANES]
                okv[h, c, out, :] = both[:, LANES:]
        remote(slq.at[blk, :, at], oq.at[:, out], lq_s.at[blk], lq_r.at[blk], partner).start()
        remote(okv.at[:, :, out], okv.at[:, :, out], lkv_s.at[blk], lkv_r.at[blk], partner).start()

    own = block(core, chip)
    near = block(core, token_chip)

    own_w = w.at[0, :, core]
    pltpu.make_async_copy(own_w, own_w, wl_sem).wait()
    other_w = w.at[0, :, other_core]
    remote(other_w, other_w, wl_s, wl_r, partner).wait_recv()

    @pl.loop(0, rows // OWN_ROWS)
    def _(i):
        local_products(0, own, pl.multiple_of(i * OWN_ROWS, OWN_ROWS), OWN_ROWS)

    for part, piece in enumerate((w_first, w_second)):
        remote(piece, piece, wx_s, wx_r.at[part], weight_peer).wait_recv()
        remote(piece, piece, wg_s, wg_r, group_peer).start()
        remote(piece, piece, wd_s.at[0], wd_r.at[0], partner).start()

    def own_products(h, c):
        @pl.loop(0, rows // OWN_ROWS)
        def _(i):
            at = pl.ds(pl.multiple_of(i * OWN_ROWS, OWN_ROWS), OWN_ROWS)
            both = product(0, at, 1, h, c)
            srq[0, c, h, at, :] = both[:, :LANES]
            srkv[0, h, c, at, :] = both[:, LANES:]
        out = pl.ds(own, rows)
        remote(srq.at[0, c, h], oq.at[h, out], oq_s, oq_r.at[core], weight_core(c)).start()
        remote(srkv.at[0, h, c], okv.at[h, c, out], okv_s, okv_r, weight_peer).start()

    other_half = 1 - half
    own_products(half, core)
    from_partner = w.at[1, half, other_core]
    remote(from_partner, from_partner, wd_s.at[0], wd_r.at[0], partner).wait_recv()
    own_products(half, other_core)
    from_group = w.at[1, other_half, core]
    remote(from_group, from_group, wg_s, wg_r, group_peer).wait_recv()
    remote(from_group, from_group, wd_s.at[1], wd_r.at[1], partner).start()
    own_products(other_half, core)
    from_both = w.at[1, other_half, other_core]
    remote(from_both, from_both, wd_s.at[1], wd_r.at[1], partner).wait_recv()
    own_products(other_half, other_core)

    @pl.loop(0, chunks)
    def _(j):
        send_n(j).wait_recv()
        start = pl.multiple_of(j * CHUNK, CHUNK)
        at = pl.ds(start, CHUNK)
        out = pl.ds(pl.multiple_of(near + start, CHUNK), CHUNK)

        @pl.loop(0, 2)
        def _(h):
            for c in range(2):
                both = product(1, at, 1, h, c)
                srq[1, c, h, at, :] = both[:, :LANES]
                srkv[1, h, c, at, :] = both[:, LANES:]
        remote(srkv.at[1, :, :, at], okv.at[:, :, out], rkv_s, rkv_r.at[j], weight_peer).start()
        for c in range(2):
            remote(srq.at[1, c, :, at], oq.at[:, out], rq_s, rq_r.at[core], weight_core(c)).start()
        local_products(1, near, start, CHUNK)

    beside = pl.ds(block(core, weight_chip), rows)
    arrived = okv.at[:, :, beside]
    remote(arrived, arrived, okv_s, okv_r, weight_peer).wait_recv()
    remote(arrived, arrived, fk_s.at[0], fk_r.at[0], partner).start()
    far = block(core, far_chip)

    @pl.loop(0, chunks)
    def _(j):
        piece = okv.at[:, :, pl.ds(pl.multiple_of(far + j * CHUNK, CHUNK), CHUNK)]
        remote(piece, piece, rkv_s, rkv_r.at[j], weight_peer).wait_recv()
        remote(piece, piece, fk_s.at[1], fk_r.at[1], partner).start()

    def all_q(c, on_chip):
        return oq.at[:, pl.ds(block(c, on_chip), rows)]

    def all_kv(c, on_chip):
        return okv.at[:, :, pl.ds(block(c, on_chip), rows)]

    for c in range(2):
        remote(all_q(c, weight_chip), all_q(c, weight_chip), oq_s, oq_r.at[c], weight_peer).wait_recv()
        remote(all_q(c, far_chip), all_q(c, far_chip), rq_s, rq_r.at[c], weight_peer).wait_recv()
    for i, on_chip in enumerate((chip, token_chip)):
        remote(all_q(other_core, on_chip), all_q(other_core, on_chip), lq_s.at[i], lq_r.at[i], partner).wait_recv()
        remote(all_kv(other_core, on_chip), all_kv(other_core, on_chip), lkv_s.at[i], lkv_r.at[i], partner).wait_recv()
    for i, on_chip in enumerate((weight_chip, far_chip)):
        remote(all_kv(other_core, on_chip), all_kv(other_core, on_chip), fk_s.at[i], fk_r.at[i], partner).wait_recv()

    def sent(ref, sem):
        remote(ref, ref, sem, n_r.at[0], partner).wait_send()

    sent(own_w, wl_s)
    sent(w.at[1, 0, 0], wx_s)
    sent(w.at[1, 0, 0], wg_s)
    for i in range(2):
        sent(w.at[1, 0, 0], wd_s.at[i])
        sent(slq.at[i], lq_s.at[i])
        sent(srkv.at[0], lkv_s.at[i])
        sent(srkv.at[0], fk_s.at[i])
    sent(n.at[0], n_s)
    sent(srq.at[0], oq_s)
    sent(srkv.at[0], okv_s)
    sent(srq.at[1], rq_s)
    sent(srkv.at[1], rkv_s)


def place(oq, okv, q, k, v, sems):
    copies = []
    for h in range(2):
        cols = pl.ds(h * LANES, LANES)
        copies.append(pltpu.make_async_copy(oq.at[h], q.at[:, cols], sems.at[h]))
        copies.append(pltpu.make_async_copy(okv.at[0, h], k.at[:, cols], sems.at[2 + h]))
        copies.append(pltpu.make_async_copy(okv.at[1, h], v.at[:, cols], sems.at[4 + h]))
    for copy in copies:
        copy.start()
    for copy in copies:
        copy.wait()


def solution(mesh):
    group_size = mesh.shape["tp"]
    chips = group_size // 2

    def local_step(x_rows, norm_gain, w_q, w_k, w_v):
        rows, depth = x_rows.shape
        head = w_q.shape[2]
        tokens = rows * group_size
        dtype = x_rows.dtype
        any_space = pl.BlockSpec(memory_space=pl.ANY)
        vmem = pl.BlockSpec(memory_space=pltpu.VMEM)
        dma = pltpu.SemaphoreType.DMA
        chunks = rows // CHUNK
        oq, okv = pl.pallas_call(
            functools.partial(exchange, chips),
            out_shape=(pltpu.VMEM((2, tokens, LANES), dtype), pltpu.VMEM((2, 2, tokens, LANES), dtype)),
            in_specs=[any_space, vmem, any_space, any_space, any_space],
            out_specs=(vmem, vmem),
            scratch_shapes=[
                pltpu.VMEM((2, rows, depth), dtype),
                pltpu.VMEM((2, 2, 2, depth, 2 * LANES), dtype),
                pltpu.VMEM((2, 2, rows, LANES), dtype),
                pltpu.VMEM((2, 2, 2, rows, LANES), dtype),
                pltpu.VMEM((2, 2, 2, rows, LANES), dtype),
                dma((chunks,)),
                dma, dma, dma,
                dma, dma((2,)),
                dma, dma,
                dma((2,)), dma((2,)),
                dma, dma((chunks,)),
                dma, dma((2,)), dma, dma,
                dma, dma((2,)), dma, dma((chunks,)),
                dma((2,)), dma((2,)), dma((2,)), dma((2,)),
                dma((2,)), dma((2,)),
            ],
            compiler_params=pltpu.CompilerParams(collective_id=0, has_side_effects=True, vmem_limit_bytes=46 * 1024 * 1024),
        )(x_rows, norm_gain.reshape(1, depth), w_q.reshape(depth, head), w_k, w_v)
        out = jax.ShapeDtypeStruct((tokens, head), dtype)
        q, k, v = pl.pallas_call(
            place,
            out_shape=(out, out, out),
            in_specs=[vmem, vmem],
            out_specs=(any_space, any_space, any_space),
            scratch_shapes=[dma((6,))],
            compiler_params=pltpu.CompilerParams(vmem_limit_bytes=1024 * 1024),
        )(pltpu.with_memory_space_constraint(oq, pltpu.VMEM), pltpu.with_memory_space_constraint(okv, pltpu.VMEM))
        return q[:, None, :], k[:, None, :], v[:, None, :]

    return jax.shard_map(local_step, mesh=mesh, in_specs=(P(("dp", "tp"), None), P(None), P(None, "tp", None), P(None, "tp"), P(None, "tp")), out_specs=(P("dp", "tp", None), P("dp", "tp", None), P("dp", "tp", None)), check_vma=False)
```

time: 284 us -> 134 us (0.47)
  waiting for transfers between devices: 175 us -> 0 us
  Pallas kernels: 0 us -> 132 us
  matrix products: 55.8 us -> 0 us
  other arithmetic: 25 us -> 0 us
  between operations: 14.1 us -> 0.64 us
  local copies, waits for them, and re-layouts: 12.7 us -> 1.31 us
    all_gather x1 -> x0, waiting for transfers between devices: 175 us -> none  [local_step(): gathered = lax.all_gather(normed, 'tp', axis=0, tiled=True)]
    pallas_call x0 -> x2, Pallas kernels: none -> 132 us  [the longest x1 127 us: local_step(): pl.pallas_call(functools.partial(exchange, chips), out_shape=(pltpu.VMEM(...]
    dot_general x3 -> x0, matrix products: 55.8 us -> none  [the longest x1 19.2 us: local_step(): jnp.dot(gathered, w_k, preferred_element_type=jnp.float32)]
    concatenate x2 -> x0, other arithmetic: 15.9 us -> none  [head_pieces(): return jnp.roll(joined, member * piece.shape[1], axis=1)]
    dynamic_slice x2 -> x0, local copies, waits for them, and re-layouts: 12.7 us -> none  [head_pieces(): return jnp.roll(joined, member * piece.shape[1], axis=1)]
    convert_element_type x1 -> x0, other arithmetic: 5.63 us -> none  [local_step(): (x_wide * lax.rsqrt(mean_sq + EPSILON) * norm_gain).astype(jnp.bfloat16)]
    reduce_sum x1 -> x0, other arithmetic: 3.46 us -> none  [local_step(): mean_sq = jnp.mean(x_wide * x_wide, axis=-1, keepdims=True)]
  transfers between devices with their start and end apart: 3 -> 0, of which waited for: 1 -> 0; matrix products, arithmetic and copies ran while one was open for 18% -> 0% of each run, Pallas kernels for 0% -> 0%
where the time goes in v1:
time: 134 us; the launch traced here: 133 us
  Pallas kernels  132 us (99%)
    pallas_call x1, Pallas kernels, local_step(): pl.pallas_call(functools.partial(exchange, chips), out_shape=(pltpu.VMEM(...  127 us
    pallas_call x1, Pallas kernels, local_step(): pl.pallas_call(place, out_shape=(out, out, out), in_specs=[vmem, vmem], o...  4.65 us

profile of v1, /device:TPU:113, one launch (start us, length us, event | category | flops | bytes accessed | tf_op | source)
XLA Modules:
  0.0 133.5 jit_solution(6775313286330492235)
XLA Ops:
  0.6 1.3 reshape.12.gain
  1.9 126.9 %shard_map.76 = (bf16[2,8192,128]{2,1,0:T(8,128)(2,1)S(1)}, bf16[2,2,8192,128]{3,2,1,0:T(8,128)(2,1)S(1)}) custom-call(bf16[1024,2304]{1,0:T(8,128)(2,1)} %x.1, f32[1,2304]{1,0:T(1,128)} %reshape.12.gain, bf16[2304,256]{1,0:T(8,128)(2,1)} %bitcast.4, bf16[2304,128]{1,0:T(8,128)(2,1)} %wk.1, bf16[2304,128]{1,0:T(8,128)(2,1)} %wv.1), custom_call_target="tpu_custom_call" | custom-call | tf_op jit(solution)/shard_map/pallas_call | solution.py:241
  128.8 4.6 %shard_map.77 = (bf16[8192,256]{1,0:T(8,128)(2,1)}, bf16[8192,256]{1,0:T(8,128)(2,1)}, bf16[8192,256]{1,0:T(8,128)(2,1)}) custom-call(bf16[2,8192,128]{2,1,0:T(8,128)(2,1)S(1)} %get-tuple-element.8.oq, bf16[2,2,8192,128]{3,2,1,0:T(8,128)(2,1)S(1)} %get-tuple-element.9.okv), custom_call_target="tpu_custom_call" | custom-call | tf_op jit(solution)/shard_map/pallas_call | solution.py:266

commit v2 on v1

--- a/solution.py
+++ b/solution.py
@@ -15,7 +15,7 @@
 MESH = pl.DeviceIdType.MESH
 
 
-def exchange(chips, x, gain, wq, wk, wv, oq, okv, n, w, slq, srq, srkv, x_sem, wl_sem, wl_s, wl_r, wx_s, wx_r, wg_s, wg_r, wd_s, wd_r, n_s, n_r,
+def exchange(chips, x, gain, wq, wk, wv, oq, okv, gain_row, n, w, slq, srq, srkv, x_sem, wl_sem, wl_s, wl_r, wx_s, wx_r, wg_s, wg_r, wd_s, wd_r, n_s, n_r,
              oq_s, oq_r, okv_s, okv_r, rq_s, rq_r, rkv_s, rkv_r, lq_s, lq_r, lkv_s, lkv_r, fk_s, fk_r):
     rows, depth = x.shape
     chunks = rows // CHUNK
@@ -51,6 +51,7 @@
     for j in range(chunks):
         load_x(j).start()
 
+    gain_row[...] = gain[...].reshape(1, depth)
     q_half = [wq.at[:, pl.ds(h * LANES, LANES)] for h in range(2)]
     kv = [wk, wv]
 
@@ -84,7 +85,7 @@
             at = pl.ds(pl.multiple_of(j * CHUNK + i * NORM_ROWS, NORM_ROWS), NORM_ROWS)
             wide = n[0, at, :].astype(jnp.float32)
             mean_sq = jnp.mean(wide * wide, axis=-1, keepdims=True)
-            n[0, at, :] = (wide * lax.rsqrt(mean_sq + EPSILON) * gain[...]).astype(jnp.bfloat16)
+            n[0, at, :] = (wide * lax.rsqrt(mean_sq + EPSILON) * gain_row[...]).astype(jnp.bfloat16)
 
         send_n(j).start()
 
@@ -120,10 +121,30 @@
     def _(i):
         local_products(0, own, pl.multiple_of(i * OWN_ROWS, OWN_ROWS), OWN_ROWS)
 
+    def own_part(h, c, part):
+        @pl.loop(0, rows // OWN_ROWS)
+        def _(i):
+            at = pl.ds(pl.multiple_of(i * OWN_ROWS, OWN_ROWS), OWN_ROWS)
+            piece = w[1, h, c, :, part * LANES:(part + 1) * LANES]
+            value = jnp.dot(n[0, at, :], piece, preferred_element_type=jnp.float32).astype(jnp.bfloat16)
+            if part == 0:
+                srq[0, c, h, at, :] = value
+            else:
+                srkv[0, h, c, at, :] = value
+
+    def send_own(h, c, part):
+        out = pl.ds(own, rows)
+        if part == 0:
+            remote(srq.at[0, c, h], oq.at[h, out], oq_s, oq_r.at[core], weight_core(c)).start()
+        else:
+            remote(srkv.at[0, h, c], okv.at[h, c, out], okv_s, okv_r, weight_peer).start()
+
     for part, piece in enumerate((w_first, w_second)):
         remote(piece, piece, wx_s, wx_r.at[part], weight_peer).wait_recv()
         remote(piece, piece, wg_s, wg_r, group_peer).start()
         remote(piece, piece, wd_s.at[0], wd_r.at[0], partner).start()
+        own_part(half, core, part)
+        send_own(half, core, part)
 
     def own_products(h, c):
         @pl.loop(0, rows // OWN_ROWS)
@@ -132,12 +153,10 @@
             both = product(0, at, 1, h, c)
             srq[0, c, h, at, :] = both[:, :LANES]
             srkv[0, h, c, at, :] = both[:, LANES:]
-        out = pl.ds(own, rows)
-        remote(srq.at[0, c, h], oq.at[h, out], oq_s, oq_r.at[core], weight_core(c)).start()
-        remote(srkv.at[0, h, c], okv.at[h, c, out], okv_s, okv_r, weight_peer).start()
+        for part in range(2):
+            send_own(h, c, part)
 
     other_half = 1 - half
-    own_products(half, core)
     from_partner = w.at[1, half, other_core]
     remote(from_partner, from_partner, wd_s.at[0], wd_r.at[0], partner).wait_recv()
     own_products(half, other_core)
@@ -244,6 +263,7 @@
             in_specs=[any_space, vmem, any_space, any_space, any_space],
             out_specs=(vmem, vmem),
             scratch_shapes=[
+                pltpu.VMEM((1, depth), norm_gain.dtype),
                 pltpu.VMEM((2, rows, depth), dtype),
                 pltpu.VMEM((2, 2, 2, depth, 2 * LANES), dtype),
                 pltpu.VMEM((2, 2, rows, LANES), dtype),
@@ -261,7 +281,7 @@
                 dma((2,)), dma((2,)),
             ],
             compiler_params=pltpu.CompilerParams(collective_id=0, has_side_effects=True, vmem_limit_bytes=46 * 1024 * 1024),
-        )(x_rows, norm_gain.reshape(1, depth), w_q.reshape(depth, head), w_k, w_v)
+        )(x_rows, norm_gain, w_q.reshape(depth, head), w_k, w_v)
         out = jax.ShapeDtypeStruct((tokens, head), dtype)
         q, k, v = pl.pallas_call(
             place,

time: 134 us -> 128 us (0.955)
  Pallas kernels: 132 us -> 128 us
    pallas_call x1, Pallas kernels: 127 us -> 123 us  [local_step(): pl.pallas_call(functools.partial(exchange, chips), out_shape=(pltpu.VMEM(...]
where the time goes in v2:
time: 128 us
  Pallas kernels  128 us (100%)
    pallas_call x1, Pallas kernels, local_step(): pl.pallas_call(functools.partial(exchange, chips), out_shape=(pltpu.VMEM(...  123 us
    pallas_call x1, Pallas kernels, local_step(): pl.pallas_call(place, out_shape=(out, out, out), in_specs=[vmem, vmem], o...  4.65 us

profile of v2, /device:TPU:113, one launch (start us, length us, event | category | flops | bytes accessed | tf_op | source)
XLA Modules:
  0.0 128.2 jit_solution(4748106869432318300)
XLA Ops:
  0.6 122.9 %shard_map.76 = (bf16[2,8192,128]{2,1,0:T(8,128)(2,1)S(1)}, bf16[2,2,8192,128]{3,2,1,0:T(8,128)(2,1)S(1)}) custom-call(bf16[1024,2304]{1,0:T(8,128)(2,1)} %x.1, f32[2304]{0:T(1024)} %gain.1, bf16[2304,256]{1,0:T(8,128)(2,1)} %bitcast.4, bf16[2304,128]{1,0:T(8,128)(2,1)} %wk.1, bf16[2304,128]{1,0:T(8,128)(2,1)} %wv.1), custom_call_target="tpu_custom_call" | custom-call | tf_op jit(solution)/shard_map/pallas_call | solution.py:260
  123.6 4.6 %shard_map.77 = (bf16[8192,256]{1,0:T(8,128)(2,1)}, bf16[8192,256]{1,0:T(8,128)(2,1)}, bf16[8192,256]{1,0:T(8,128)(2,1)}) custom-call(bf16[2,8192,128]{2,1,0:T(8,128)(2,1)S(1)} %get-tuple-element.8.oq, bf16[2,2,8192,128]{3,2,1,0:T(8,128)(2,1)S(1)} %get-tuple-element.9.okv), custom_call_target="tpu_custom_call" | custom-call | tf_op jit(solution)/shard_map/pallas_call | solution.py:286

commit v3 on v2

--- a/solution.py
+++ b/solution.py
@@ -12,10 +12,11 @@
 NORM_ROWS = 32
 CHUNK = 128
 OWN_ROWS = 256
+PLACE_BLOCKS = 4
 MESH = pl.DeviceIdType.MESH
 
 
-def exchange(chips, x, gain, wq, wk, wv, oq, okv, gain_row, n, w, slq, srq, srkv, x_sem, wl_sem, wl_s, wl_r, wx_s, wx_r, wg_s, wg_r, wd_s, wd_r, n_s, n_r,
+def exchange(chips, x, gain, wq, wk, wv, oq, okv, gain_copy, gain_row, n, w, slq, srq, srkv, g_sem, x_sem, wl_sem, wl_s, wl_r, wx_s, wx_r, wg_s, wg_r, wd_s, wd_r, n_s, n_r,
              oq_s, oq_r, okv_s, okv_r, rq_s, rq_r, rkv_s, rkv_r, lq_s, lq_r, lkv_s, lkv_r, fk_s, fk_r):
     rows, depth = x.shape
     chunks = rows // CHUNK
@@ -48,30 +49,40 @@
     def load_x(j):
         return pltpu.make_async_copy(x.at[chunk_of(j)], n.at[0, chunk_of(j)], x_sem.at[j])
 
-    for j in range(chunks):
-        load_x(j).start()
-
-    gain_row[...] = gain[...].reshape(1, depth)
     q_half = [wq.at[:, pl.ds(h * LANES, LANES)] for h in range(2)]
     kv = [wk, wv]
+
+    def own_w_part(h, part):
+        return w.at[0, h, core, :, pl.ds(part * LANES, LANES)]
 
     barrier = pltpu.get_barrier_semaphore()
     for peer in (partner, token_peer, weight_peer, weight_core(other_core), group_peer):
         pl.semaphore_signal(barrier, inc=1, device_id=peer, device_id_type=MESH)
+    first = own_w_part(half, 0)
+    pltpu.make_async_copy(wq.at[:, pl.ds(pl.multiple_of(half * LANES, LANES), LANES)], first, wl_sem.at[0]).start()
+    second = own_w_part(1 - half, 0)
+    pltpu.make_async_copy(wq.at[:, pl.ds(pl.multiple_of((1 - half) * LANES, LANES), LANES)], second, wl_sem.at[1]).start()
+    for h in range(2):
+        pltpu.make_async_copy(kv[h], own_w_part(h, 1), wl_sem.at[2 + h]).start()
+    gain_load = pltpu.make_async_copy(gain, gain_copy, g_sem)
+    gain_load.start()
+    for j in range(chunks):
+        load_x(j).start()
+    pltpu.make_async_copy(first, first, wl_sem.at[0]).wait()
     pl.semaphore_wait(barrier, 5)
 
     w_first = w.at[1, half, core, :, pl.ds(0, LANES)]
     w_second = w.at[1, half, core, :, pl.ds(LANES, LANES)]
-    remote(wq.at[:, pl.ds(pl.multiple_of(half * LANES, LANES), LANES)], w_first, wx_s, wx_r.at[0], weight_peer).start()
+    remote(first, w_first, wx_s, wx_r.at[0], weight_peer).start()
     for h in range(2):
         @pl.when(half == h)
         def _():
             remote(kv[h], w_second, wx_s, wx_r.at[1], weight_peer).start()
     for h in range(2):
         for part, src in enumerate((q_half[h], kv[h])):
-            dst = w.at[0, h, core, :, pl.ds(part * LANES, LANES)]
-            remote(src, dst, wl_s, wl_r, partner).start()
-            pltpu.make_async_copy(src, dst, wl_sem).start()
+            remote(src, own_w_part(h, part), wl_s, wl_r, partner).start()
+    gain_load.wait()
+    gain_row[...] = gain_copy[...].reshape(1, depth)
 
     def send_n(j):
         return remote(n.at[0, chunk_of(j)], n.at[1, chunk_of(j)], n_s, n_r.at[j], token_peer)
@@ -113,7 +124,9 @@
     near = block(core, token_chip)
 
     own_w = w.at[0, :, core]
-    pltpu.make_async_copy(own_w, own_w, wl_sem).wait()
+    pltpu.make_async_copy(second, second, wl_sem.at[1]).wait()
+    for h in range(2):
+        pltpu.make_async_copy(kv[h], own_w_part(h, 1), wl_sem.at[2 + h]).wait()
     other_w = w.at[0, :, other_core]
     remote(other_w, other_w, wl_s, wl_r, partner).wait_recv()
 
@@ -232,12 +245,14 @@
 
 
 def place(oq, okv, q, k, v, sems):
+    rows = oq.shape[1] // PLACE_BLOCKS
     copies = []
-    for h in range(2):
-        cols = pl.ds(h * LANES, LANES)
-        copies.append(pltpu.make_async_copy(oq.at[h], q.at[:, cols], sems.at[h]))
-        copies.append(pltpu.make_async_copy(okv.at[0, h], k.at[:, cols], sems.at[2 + h]))
-        copies.append(pltpu.make_async_copy(okv.at[1, h], v.at[:, cols], sems.at[4 + h]))
+    for i in range(PLACE_BLOCKS):
+        at = pl.ds(i * rows, rows)
+        for h in range(2):
+            cols = pl.ds(h * LANES, LANES)
+            for a, (src, dst) in enumerate(((oq, q), (okv.at[0], k), (okv.at[1], v))):
+                copies.append(pltpu.make_async_copy(src.at[h, at], dst.at[at, cols], sems.at[i, h, a]))
     for copy in copies:
         copy.start()
     for copy in copies:
@@ -260,17 +275,18 @@
         oq, okv = pl.pallas_call(
             functools.partial(exchange, chips),
             out_shape=(pltpu.VMEM((2, tokens, LANES), dtype), pltpu.VMEM((2, 2, tokens, LANES), dtype)),
-            in_specs=[any_space, vmem, any_space, any_space, any_space],
+            in_specs=[any_space] * 5,
             out_specs=(vmem, vmem),
             scratch_shapes=[
+                pltpu.VMEM((depth,), norm_gain.dtype),
                 pltpu.VMEM((1, depth), norm_gain.dtype),
                 pltpu.VMEM((2, rows, depth), dtype),
                 pltpu.VMEM((2, 2, 2, depth, 2 * LANES), dtype),
                 pltpu.VMEM((2, 2, rows, LANES), dtype),
                 pltpu.VMEM((2, 2, 2, rows, LANES), dtype),
                 pltpu.VMEM((2, 2, 2, rows, LANES), dtype),
-                dma((chunks,)),
-                dma, dma, dma,
+                dma, dma((chunks,)),
+                dma((4,)), dma, dma,
                 dma, dma((2,)),
                 dma, dma,
                 dma((2,)), dma((2,)),
@@ -288,7 +304,7 @@
             out_shape=(out, out, out),
             in_specs=[vmem, vmem],
             out_specs=(any_space, any_space, any_space),
-            scratch_shapes=[dma((6,))],
+            scratch_shapes=[dma((PLACE_BLOCKS, 2, 3))],
             compiler_params=pltpu.CompilerParams(vmem_limit_bytes=1024 * 1024),
         )(pltpu.with_memory_space_constraint(oq, pltpu.VMEM), pltpu.with_memory_space_constraint(okv, pltpu.VMEM))
         return q[:, None, :], k[:, None, :], v[:, None, :]

time: 128 us -> 128 us (level)
  no operation moved by 1% of the time
where the time goes in v3:
time: 128 us
  Pallas kernels  127 us (99%)
    pallas_call x1, Pallas kernels, local_step(): pl.pallas_call(functools.partial(exchange, chips), out_shape=(pltpu.VMEM(...  122 us
    pallas_call x1, Pallas kernels, local_step(): pl.pallas_call(place, out_shape=(out, out, out), in_specs=[vmem, vmem], o...  4.75 us

profile of v3, /device:TPU:113, one launch (start us, length us, event | category | flops | bytes accessed | tf_op | source)
XLA Modules:
  0.0 127.8 jit_solution(769138828445069252)
XLA Ops:
  0.6 122.4 %shard_map.76 = (bf16[2,8192,128]{2,1,0:T(8,128)(2,1)S(1)}, bf16[2,2,8192,128]{3,2,1,0:T(8,128)(2,1)S(1)}) custom-call(bf16[1024,2304]{1,0:T(8,128)(2,1)} %x.1, f32[2304]{0:T(1024)} %gain.1, bf16[2304,256]{1,0:T(8,128)(2,1)} %bitcast.4, bf16[2304,128]{1,0:T(8,128)(2,1)} %wk.1, bf16[2304,128]{1,0:T(8,128)(2,1)} %wv.1), custom_call_target="tpu_custom_call" | custom-call | tf_op jit(solution)/shard_map/pallas_call | solution.py:275
  123.0 4.7 %shard_map.77 = (bf16[8192,256]{1,0:T(8,128)(2,1)}, bf16[8192,256]{1,0:T(8,128)(2,1)}, bf16[8192,256]{1,0:T(8,128)(2,1)}) custom-call(bf16[2,8192,128]{2,1,0:T(8,128)(2,1)S(1)} %get-tuple-element.8.oq, bf16[2,2,8192,128]{3,2,1,0:T(8,128)(2,1)S(1)} %get-tuple-element.9.okv), custom_call_target="tpu_custom_call" | custom-call | tf_op jit(solution)/shard_map/pallas_call | solution.py:302

commit v4 on v3

--- a/solution.py
+++ b/solution.py
@@ -12,7 +12,7 @@
 NORM_ROWS = 32
 CHUNK = 128
 OWN_ROWS = 256
-PLACE_BLOCKS = 4
+PLACE_BLOCKS = 1
 MESH = pl.DeviceIdType.MESH
 
 
@@ -25,9 +25,9 @@
     half = lax.rem(group, 2)
     core = lax.rem(device, 2)
     chip = lax.div(device, 2)
-    token_chip = chip + 1 - 2 * lax.rem(chip, 2)
-    weight_chip = chips - 1 - chip
-    far_chip = weight_chip + 1 - 2 * lax.rem(weight_chip, 2)
+    token_chip = chips - 1 - chip
+    weight_chip = chip + 1 - 2 * lax.rem(chip, 2)
+    far_chip = chips - 1 - weight_chip
     other_core = 1 - core
     partner = {"tp": 2 * chip + other_core}
     token_peer = {"tp": 2 * token_chip + core}

time: 128 us -> 126 us (0.984)
  Pallas kernels: 127 us -> 125 us
    pallas_call x1, Pallas kernels: 122 us -> 121 us  [local_step(): pl.pallas_call(functools.partial(exchange, chips), out_shape=(pltpu.VMEM(...]
where the time goes in v4:
time: 126 us
  Pallas kernels  125 us (99%)
    pallas_call x1, Pallas kernels, local_step(): pl.pallas_call(functools.partial(exchange, chips), out_shape=(pltpu.VMEM(...  121 us
    pallas_call x1, Pallas kernels, local_step(): pl.pallas_call(place, out_shape=(out, out, out), in_specs=[vmem, vmem], o...  4.65 us

profile of v4, /device:TPU:113, one launch (start us, length us, event | category | flops | bytes accessed | tf_op | source)
XLA Modules:
  0.0 126.1 jit_solution(11661183330543211017)
XLA Ops:
  0.6 120.8 %shard_map.76 = (bf16[2,8192,128]{2,1,0:T(8,128)(2,1)S(1)}, bf16[2,2,8192,128]{3,2,1,0:T(8,128)(2,1)S(1)}) custom-call(bf16[1024,2304]{1,0:T(8,128)(2,1)} %x.1, f32[2304]{0:T(1024)} %gain.1, bf16[2304,256]{1,0:T(8,128)(2,1)} %bitcast.4, bf16[2304,128]{1,0:T(8,128)(2,1)} %wk.1, bf16[2304,128]{1,0:T(8,128)(2,1)} %wv.1), custom_call_target="tpu_custom_call" | custom-call | tf_op jit(solution)/shard_map/pallas_call | solution.py:275
  121.5 4.6 %shard_map.77 = (bf16[8192,256]{1,0:T(8,128)(2,1)}, bf16[8192,256]{1,0:T(8,128)(2,1)}, bf16[8192,256]{1,0:T(8,128)(2,1)}) custom-call(bf16[2,8192,128]{2,1,0:T(8,128)(2,1)S(1)} %get-tuple-element.8.oq, bf16[2,2,8192,128]{3,2,1,0:T(8,128)(2,1)S(1)} %get-tuple-element.9.okv), custom_call_target="tpu_custom_call" | custom-call | tf_op jit(solution)/shard_map/pallas_call | solution.py:302

commit v5 on v4

--- a/solution.py
+++ b/solution.py
@@ -13,10 +13,11 @@
 CHUNK = 128
 OWN_ROWS = 256
 PLACE_BLOCKS = 1
+W_BLOCKS = 4
 MESH = pl.DeviceIdType.MESH
 
 
-def exchange(chips, x, gain, wq, wk, wv, oq, okv, gain_copy, gain_row, n, w, slq, srq, srkv, g_sem, x_sem, wl_sem, wl_s, wl_r, wx_s, wx_r, wg_s, wg_r, wd_s, wd_r, n_s, n_r,
+def exchange(chips, x, gain, wq, wk, wv, oq, okv, gain_copy, gain_row, n, w, slq, srq, srkv, g_sem, x_sem, w0_sem, wl_sem, wl_s, wl_r, wx_s, wx_r, wg_s, wg_r, wd_s, wd_r, n_s, n_r,
              oq_s, oq_r, okv_s, okv_r, rq_s, rq_r, rkv_s, rkv_r, lq_s, lq_r, lkv_s, lkv_r, fk_s, fk_r):
     rows, depth = x.shape
     chunks = rows // CHUNK
@@ -55,29 +56,37 @@
     def own_w_part(h, part):
         return w.at[0, h, core, :, pl.ds(part * LANES, LANES)]
 
+    w_rows = depth // W_BLOCKS
+
+    def at_rows(ref, r):
+        return ref.at[pl.ds(r * w_rows, w_rows)]
+
     barrier = pltpu.get_barrier_semaphore()
     for peer in (partner, token_peer, weight_peer, weight_core(other_core), group_peer):
         pl.semaphore_signal(barrier, inc=1, device_id=peer, device_id_type=MESH)
     first = own_w_part(half, 0)
-    pltpu.make_async_copy(wq.at[:, pl.ds(pl.multiple_of(half * LANES, LANES), LANES)], first, wl_sem.at[0]).start()
+    first_src = wq.at[:, pl.ds(pl.multiple_of(half * LANES, LANES), LANES)]
+    for r in range(W_BLOCKS):
+        pltpu.make_async_copy(at_rows(first_src, r), at_rows(first, r), w0_sem.at[r]).start()
     second = own_w_part(1 - half, 0)
-    pltpu.make_async_copy(wq.at[:, pl.ds(pl.multiple_of((1 - half) * LANES, LANES), LANES)], second, wl_sem.at[1]).start()
+    pltpu.make_async_copy(wq.at[:, pl.ds(pl.multiple_of((1 - half) * LANES, LANES), LANES)], second, wl_sem.at[0]).start()
     for h in range(2):
-        pltpu.make_async_copy(kv[h], own_w_part(h, 1), wl_sem.at[2 + h]).start()
+        pltpu.make_async_copy(kv[h], own_w_part(h, 1), wl_sem.at[1 + h]).start()
     gain_load = pltpu.make_async_copy(gain, gain_copy, g_sem)
     gain_load.start()
     for j in range(chunks):
         load_x(j).start()
-    pltpu.make_async_copy(first, first, wl_sem.at[0]).wait()
     pl.semaphore_wait(barrier, 5)
 
-    w_first = w.at[1, half, core, :, pl.ds(0, LANES)]
-    w_second = w.at[1, half, core, :, pl.ds(LANES, LANES)]
-    remote(first, w_first, wx_s, wx_r.at[0], weight_peer).start()
+    w_parts = [w.at[1, half, core, :, pl.ds(part * LANES, LANES)] for part in range(2)]
+    for r in range(W_BLOCKS):
+        pltpu.make_async_copy(at_rows(first, r), at_rows(first, r), w0_sem.at[r]).wait()
+        remote(at_rows(first, r), at_rows(w_parts[0], r), wx_s, wx_r.at[0, r], weight_peer).start()
     for h in range(2):
         @pl.when(half == h)
         def _():
-            remote(kv[h], w_second, wx_s, wx_r.at[1], weight_peer).start()
+            for r in range(W_BLOCKS):
+                remote(at_rows(kv[h], r), at_rows(w_parts[1], r), wx_s, wx_r.at[1, r], weight_peer).start()
     for h in range(2):
         for part, src in enumerate((q_half[h], kv[h])):
             remote(src, own_w_part(h, part), wl_s, wl_r, partner).start()
@@ -124,15 +133,11 @@
     near = block(core, token_chip)
 
     own_w = w.at[0, :, core]
-    pltpu.make_async_copy(second, second, wl_sem.at[1]).wait()
+    pltpu.make_async_copy(second, second, wl_sem.at[0]).wait()
     for h in range(2):
-        pltpu.make_async_copy(kv[h], own_w_part(h, 1), wl_sem.at[2 + h]).wait()
+        pltpu.make_async_copy(kv[h], own_w_part(h, 1), wl_sem.at[1 + h]).wait()
     other_w = w.at[0, :, other_core]
     remote(other_w, other_w, wl_s, wl_r, partner).wait_recv()
-
-    @pl.loop(0, rows // OWN_ROWS)
-    def _(i):
-        local_products(0, own, pl.multiple_of(i * OWN_ROWS, OWN_ROWS), OWN_ROWS)
 
     def own_part(h, c, part):
         @pl.loop(0, rows // OWN_ROWS)
@@ -152,12 +157,19 @@
         else:
             remote(srkv.at[0, h, c], okv.at[h, c, out], okv_s, okv_r, weight_peer).start()
 
-    for part, piece in enumerate((w_first, w_second)):
-        remote(piece, piece, wx_s, wx_r.at[part], weight_peer).wait_recv()
+    local_chunks = rows // OWN_ROWS
+    steps = 2 * W_BLOCKS
+    for step in range(steps):
+        part, r = divmod(step, W_BLOCKS)
+        piece = at_rows(w_parts[part], r)
+        remote(piece, piece, wx_s, wx_r.at[part, r], weight_peer).wait_recv()
         remote(piece, piece, wg_s, wg_r, group_peer).start()
         remote(piece, piece, wd_s.at[0], wd_r.at[0], partner).start()
-        own_part(half, core, part)
-        send_own(half, core, part)
+        if r == W_BLOCKS - 1:
+            own_part(half, core, part)
+            send_own(half, core, part)
+        for i in range(step * local_chunks // steps, (step + 1) * local_chunks // steps):
+            local_products(0, own, i * OWN_ROWS, OWN_ROWS)
 
     def own_products(h, c):
         @pl.loop(0, rows // OWN_ROWS)
@@ -286,8 +298,8 @@
                 pltpu.VMEM((2, 2, 2, rows, LANES), dtype),
                 pltpu.VMEM((2, 2, 2, rows, LANES), dtype),
                 dma, dma((chunks,)),
-                dma((4,)), dma, dma,
-                dma, dma((2,)),
+                dma((W_BLOCKS,)), dma((3,)), dma, dma,
+                dma, dma((2, W_BLOCKS)),
                 dma, dma,
                 dma((2,)), dma((2,)),
                 dma, dma((chunks,)),

time: 126 us -> 126 us (level)
  no operation moved by 1% of the time
where the time goes in v5:
time: 126 us
  Pallas kernels  126 us (100%)
    pallas_call x1, Pallas kernels, local_step(): pl.pallas_call(functools.partial(exchange, chips), out_shape=(pltpu.VMEM(...  121 us
    pallas_call x1, Pallas kernels, local_step(): pl.pallas_call(place, out_shape=(out, out, out), in_specs=[vmem, vmem], o...  4.65 us

profile of v5, /device:TPU:113, one launch (start us, length us, event | category | flops | bytes accessed | tf_op | source)
XLA Modules:
  0.0 126.2 jit_solution(4273506621143467640)
XLA Ops:
  0.6 120.9 %shard_map.76 = (bf16[2,8192,128]{2,1,0:T(8,128)(2,1)S(1)}, bf16[2,2,8192,128]{3,2,1,0:T(8,128)(2,1)S(1)}) custom-call(bf16[1024,2304]{1,0:T(8,128)(2,1)} %x.1, f32[2304]{0:T(1024)} %gain.1, bf16[2304,256]{1,0:T(8,128)(2,1)} %bitcast.4, bf16[2304,128]{1,0:T(8,128)(2,1)} %wk.1, bf16[2304,128]{1,0:T(8,128)(2,1)} %wv.1), custom_call_target="tpu_custom_call" | custom-call | tf_op jit(solution)/shard_map/pallas_call | solution.py:287
  121.6 4.6 %shard_map.77 = (bf16[8192,256]{1,0:T(8,128)(2,1)}, bf16[8192,256]{1,0:T(8,128)(2,1)}, bf16[8192,256]{1,0:T(8,128)(2,1)}) custom-call(bf16[2,8192,128]{2,1,0:T(8,128)(2,1)S(1)} %get-tuple-element.8.oq, bf16[2,2,8192,128]{3,2,1,0:T(8,128)(2,1)S(1)} %get-tuple-element.9.okv), custom_call_target="tpu_custom_call" | custom-call | tf_op jit(solution)/shard_map/pallas_call | solution.py:314

commit v6 on v5

--- a/solution.py
+++ b/solution.py
@@ -12,8 +12,8 @@
 NORM_ROWS = 32
 CHUNK = 128
 OWN_ROWS = 256
-PLACE_BLOCKS = 1
-W_BLOCKS = 4
+PLACE_BLOCKS = 2
+W_BLOCKS = 2
 MESH = pl.DeviceIdType.MESH
 
 
@@ -35,6 +35,9 @@
     weight_peer = {"tp": 2 * weight_chip + core}
     group_peer = {"dp": group + 1 - 2 * half}
 
+    def lanes(i):
+        return pl.ds(pl.multiple_of(i * LANES, LANES), LANES)
+
     def weight_core(c):
         return {"tp": 2 * weight_chip + c}
 
@@ -122,12 +125,12 @@
                 c = lax.rem(core + b, 2)
                 both = product(blk, at, 0, h, c)
                 if b == 0:
-                    oq[h, out, :] = both[:, :LANES]
+                    oq[out, lanes(h)] = both[:, :LANES]
                 else:
-                    slq[blk, h, at, :] = both[:, :LANES]
-                okv[h, c, out, :] = both[:, LANES:]
-        remote(slq.at[blk, :, at], oq.at[:, out], lq_s.at[blk], lq_r.at[blk], partner).start()
-        remote(okv.at[:, :, out], okv.at[:, :, out], lkv_s.at[blk], lkv_r.at[blk], partner).start()
+                    slq[blk, at, lanes(h)] = both[:, :LANES]
+                okv[h, out, lanes(c)] = both[:, LANES:]
+        remote(slq.at[blk, at], oq.at[out], lq_s.at[blk], lq_r.at[blk], partner).start()
+        remote(okv.at[:, out], okv.at[:, out], lkv_s.at[blk], lkv_r.at[blk], partner).start()
 
     own = block(core, chip)
     near = block(core, token_chip)
@@ -146,16 +149,16 @@
             piece = w[1, h, c, :, part * LANES:(part + 1) * LANES]
             value = jnp.dot(n[0, at, :], piece, preferred_element_type=jnp.float32).astype(jnp.bfloat16)
             if part == 0:
-                srq[0, c, h, at, :] = value
+                srq[0, c, at, lanes(h)] = value
             else:
-                srkv[0, h, c, at, :] = value
+                srkv[0, h, at, lanes(c)] = value
 
     def send_own(h, c, part):
         out = pl.ds(own, rows)
         if part == 0:
-            remote(srq.at[0, c, h], oq.at[h, out], oq_s, oq_r.at[core], weight_core(c)).start()
+            remote(srq.at[0, c, :, lanes(h)], oq.at[out, lanes(h)], oq_s, oq_r.at[core], weight_core(c)).start()
         else:
-            remote(srkv.at[0, h, c], okv.at[h, c, out], okv_s, okv_r, weight_peer).start()
+            remote(srkv.at[0, h, :, lanes(c)], okv.at[h, out, lanes(c)], okv_s, okv_r, weight_peer).start()
 
     local_chunks = rows // OWN_ROWS
     steps = 2 * W_BLOCKS
@@ -176,8 +179,8 @@
         def _(i):
             at = pl.ds(pl.multiple_of(i * OWN_ROWS, OWN_ROWS), OWN_ROWS)
             both = product(0, at, 1, h, c)
-            srq[0, c, h, at, :] = both[:, :LANES]
-            srkv[0, h, c, at, :] = both[:, LANES:]
+            srq[0, c, at, lanes(h)] = both[:, :LANES]
+            srkv[0, h, at, lanes(c)] = both[:, LANES:]
         for part in range(2):
             send_own(h, c, part)
 
@@ -204,30 +207,30 @@
         def _(h):
             for c in range(2):
                 both = product(1, at, 1, h, c)
-                srq[1, c, h, at, :] = both[:, :LANES]
-                srkv[1, h, c, at, :] = both[:, LANES:]
-        remote(srkv.at[1, :, :, at], okv.at[:, :, out], rkv_s, rkv_r.at[j], weight_peer).start()
+                srq[1, c, at, lanes(h)] = both[:, :LANES]
+                srkv[1, h, at, lanes(c)] = both[:, LANES:]
+        remote(srkv.at[1, :, at], okv.at[:, out], rkv_s, rkv_r.at[j], weight_peer).start()
         for c in range(2):
-            remote(srq.at[1, c, :, at], oq.at[:, out], rq_s, rq_r.at[core], weight_core(c)).start()
+            remote(srq.at[1, c, at], oq.at[out], rq_s, rq_r.at[core], weight_core(c)).start()
         local_products(1, near, start, CHUNK)
 
     beside = pl.ds(block(core, weight_chip), rows)
-    arrived = okv.at[:, :, beside]
+    arrived = okv.at[:, beside]
     remote(arrived, arrived, okv_s, okv_r, weight_peer).wait_recv()
     remote(arrived, arrived, fk_s.at[0], fk_r.at[0], partner).start()
     far = block(core, far_chip)
 
     @pl.loop(0, chunks)
     def _(j):
-        piece = okv.at[:, :, pl.ds(pl.multiple_of(far + j * CHUNK, CHUNK), CHUNK)]
+        piece = okv.at[:, pl.ds(pl.multiple_of(far + j * CHUNK, CHUNK), CHUNK)]
         remote(piece, piece, rkv_s, rkv_r.at[j], weight_peer).wait_recv()
         remote(piece, piece, fk_s.at[1], fk_r.at[1], partner).start()
 
     def all_q(c, on_chip):
-        return oq.at[:, pl.ds(block(c, on_chip), rows)]
+        return oq.at[pl.ds(block(c, on_chip), rows)]
 
     def all_kv(c, on_chip):
-        return okv.at[:, :, pl.ds(block(c, on_chip), rows)]
+        return okv.at[:, pl.ds(block(c, on_chip), rows)]
 
     for c in range(2):
         remote(all_q(c, weight_chip), all_q(c, weight_chip), oq_s, oq_r.at[c], weight_peer).wait_recv()
@@ -257,14 +260,12 @@
 
 
 def place(oq, okv, q, k, v, sems):
-    rows = oq.shape[1] // PLACE_BLOCKS
+    rows = oq.shape[0] // PLACE_BLOCKS
     copies = []
     for i in range(PLACE_BLOCKS):
         at = pl.ds(i * rows, rows)
-        for h in range(2):
-            cols = pl.ds(h * LANES, LANES)
-            for a, (src, dst) in enumerate(((oq, q), (okv.at[0], k), (okv.at[1], v))):
-                copies.append(pltpu.make_async_copy(src.at[h, at], dst.at[at, cols], sems.at[i, h, a]))
+        for a, (src, dst) in enumerate(((oq, q), (okv.at[0], k), (okv.at[1], v))):
+            copies.append(pltpu.make_async_copy(src.at[at], dst.at[at], sems.at[i, a]))
     for copy in copies:
         copy.start()
     for copy in copies:
@@ -286,7 +287,7 @@
         chunks = rows // CHUNK
         oq, okv = pl.pallas_call(
             functools.partial(exchange, chips),
-            out_shape=(pltpu.VMEM((2, tokens, LANES), dtype), pltpu.VMEM((2, 2, tokens, LANES), dtype)),
+            out_shape=(pltpu.VMEM((tokens, head), dtype), pltpu.VMEM((2, tokens, head), dtype)),
             in_specs=[any_space] * 5,
             out_specs=(vmem, vmem),
             scratch_shapes=[
@@ -294,9 +295,9 @@
                 pltpu.VMEM((1, depth), norm_gain.dtype),
                 pltpu.VMEM((2, rows, depth), dtype),
                 pltpu.VMEM((2, 2, 2, depth, 2 * LANES), dtype),
-                pltpu.VMEM((2, 2, rows, LANES), dtype),
-                pltpu.VMEM((2, 2, 2, rows, LANES), dtype),
-                pltpu.VMEM((2, 2, 2, rows, LANES), dtype),
+                pltpu.VMEM((2, rows, head), dtype),
+                pltpu.VMEM((2, 2, rows, head), dtype),
+                pltpu.VMEM((2, 2, rows, head), dtype),
                 dma, dma((chunks,)),
                 dma((W_BLOCKS,)), dma((3,)), dma, dma,
                 dma, dma((2, W_BLOCKS)),
@@ -316,7 +317,7 @@
             out_shape=(out, out, out),
             in_specs=[vmem, vmem],
             out_specs=(any_space, any_space, any_space),
-            scratch_shapes=[dma((PLACE_BLOCKS, 2, 3))],
+            scratch_shapes=[dma((PLACE_BLOCKS, 3))],
             compiler_params=pltpu.CompilerParams(vmem_limit_bytes=1024 * 1024),
         )(pltpu.with_memory_space_constraint(oq, pltpu.VMEM), pltpu.with_memory_space_constraint(okv, pltpu.VMEM))
         return q[:, None, :], k[:, None, :], v[:, None, :]

time: 126 us -> 126 us (level)
  no operation moved by 1% of the time
where the time goes in v6:
time: 126 us
  Pallas kernels  126 us (100%)
    pallas_call x1, Pallas kernels, local_step(): pl.pallas_call(functools.partial(exchange, chips), out_shape=(pltpu.VMEM(...  121 us
    pallas_call x1, Pallas kernels, local_step(): pl.pallas_call(place, out_shape=(out, out, out), in_specs=[vmem, vmem], o...  4.65 us

profile of v6, /device:TPU:113, one launch (start us, length us, event | category | flops | bytes accessed | tf_op | source)
XLA Modules:
  0.0 126.1 jit_solution(11671667709847756554)
XLA Ops:
  0.6 120.9 %shard_map.76 = (bf16[8192,256]{1,0:T(8,128)(2,1)S(1)}, bf16[2,8192,256]{2,1,0:T(8,128)(2,1)S(1)}) custom-call(bf16[1024,2304]{1,0:T(8,128)(2,1)} %x.1, f32[2304]{0:T(1024)} %gain.1, bf16[2304,256]{1,0:T(8,128)(2,1)} %bitcast.4, bf16[2304,128]{1,0:T(8,128)(2,1)} %wk.1, bf16[2304,128]{1,0:T(8,128)(2,1)} %wv.1), custom_call_target="tpu_custom_call" | custom-call | tf_op jit(solution)/shard_map/pallas_call | solution.py:288
  121.5 4.6 %shard_map.77 = (bf16[8192,256]{1,0:T(8,128)(2,1)}, bf16[8192,256]{1,0:T(8,128)(2,1)}, bf16[8192,256]{1,0:T(8,128)(2,1)}) custom-call(bf16[8192,256]{1,0:T(8,128)(2,1)S(1)} %get-tuple-element.8.oq, bf16[2,8192,256]{2,1,0:T(8,128)(2,1)S(1)} %get-tuple-element.9.okv), custom_call_target="tpu_custom_call" | custom-call | tf_op jit(solution)/shard_map/pallas_call | solution.py:315

commit v7 on v6

--- a/solution.py
+++ b/solution.py
@@ -14,6 +14,7 @@
 OWN_ROWS = 256
 PLACE_BLOCKS = 2
 W_BLOCKS = 2
+W_FIRST = 256
 MESH = pl.DeviceIdType.MESH
 
 
@@ -59,18 +60,23 @@
     def own_w_part(h, part):
         return w.at[0, h, core, :, pl.ds(part * LANES, LANES)]
 
-    w_rows = depth // W_BLOCKS
-
-    def at_rows(ref, r):
-        return ref.at[pl.ds(r * w_rows, w_rows)]
+    cuts = ((0, W_FIRST, depth), (0, depth // 2, depth))
+
+    def at_rows(ref, part, r):
+        return ref.at[pl.ds(cuts[part][r], cuts[part][r + 1] - cuts[part][r])]
 
     barrier = pltpu.get_barrier_semaphore()
-    for peer in (partner, token_peer, weight_peer, weight_core(other_core), group_peer):
-        pl.semaphore_signal(barrier, inc=1, device_id=peer, device_id_type=MESH)
+
+    def greet(peers):
+        for peer in peers:
+            pl.semaphore_signal(barrier, inc=1, device_id=peer, device_id_type=MESH)
+
+    greet((partner, weight_peer, weight_core(other_core)))
+    follows = lax.div(2 * chip, chips) + half
     first = own_w_part(half, 0)
     first_src = wq.at[:, pl.ds(pl.multiple_of(half * LANES, LANES), LANES)]
     for r in range(W_BLOCKS):
-        pltpu.make_async_copy(at_rows(first_src, r), at_rows(first, r), w0_sem.at[r]).start()
+        pltpu.make_async_copy(at_rows(first_src, 0, r), at_rows(first, 0, r), w0_sem.at[r]).start()
     second = own_w_part(1 - half, 0)
     pltpu.make_async_copy(wq.at[:, pl.ds(pl.multiple_of((1 - half) * LANES, LANES), LANES)], second, wl_sem.at[0]).start()
     for h in range(2):
@@ -79,17 +85,18 @@
     gain_load.start()
     for j in range(chunks):
         load_x(j).start()
-    pl.semaphore_wait(barrier, 5)
+    pl.semaphore_wait(barrier, 3 + follows)
+    greet((token_peer, group_peer))
 
     w_parts = [w.at[1, half, core, :, pl.ds(part * LANES, LANES)] for part in range(2)]
     for r in range(W_BLOCKS):
-        pltpu.make_async_copy(at_rows(first, r), at_rows(first, r), w0_sem.at[r]).wait()
-        remote(at_rows(first, r), at_rows(w_parts[0], r), wx_s, wx_r.at[0, r], weight_peer).start()
+        pltpu.make_async_copy(at_rows(first, 0, r), at_rows(first, 0, r), w0_sem.at[r]).wait()
+        remote(at_rows(first, 0, r), at_rows(w_parts[0], 0, r), wx_s, wx_r.at[0, r], weight_peer).start()
     for h in range(2):
         @pl.when(half == h)
         def _():
             for r in range(W_BLOCKS):
-                remote(at_rows(kv[h], r), at_rows(w_parts[1], r), wx_s, wx_r.at[1, r], weight_peer).start()
+                remote(at_rows(kv[h], 1, r), at_rows(w_parts[1], 1, r), wx_s, wx_r.at[1, r], weight_peer).start()
     for h in range(2):
         for part, src in enumerate((q_half[h], kv[h])):
             remote(src, own_w_part(h, part), wl_s, wl_r, partner).start()
@@ -109,6 +116,10 @@
             wide = n[0, at, :].astype(jnp.float32)
             mean_sq = jnp.mean(wide * wide, axis=-1, keepdims=True)
             n[0, at, :] = (wide * lax.rsqrt(mean_sq + EPSILON) * gain_row[...]).astype(jnp.bfloat16)
+
+        @pl.when(jnp.logical_and(j == 0, follows < 2))
+        def _():
+            pl.semaphore_wait(barrier, 2 - follows)
 
         send_n(j).start()
 
@@ -164,7 +175,7 @@
     steps = 2 * W_BLOCKS
     for step in range(steps):
         part, r = divmod(step, W_BLOCKS)
-        piece = at_rows(w_parts[part], r)
+        piece = at_rows(w_parts[part], part, r)
         remote(piece, piece, wx_s, wx_r.at[part, r], weight_peer).wait_recv()
         remote(piece, piece, wg_s, wg_r, group_peer).start()
         remote(piece, piece, wd_s.at[0], wd_r.at[0], partner).start()

time: 126 us -> 126 us (level)
  no operation moved by 1% of the time
where the time goes in v7:
time: 126 us
  Pallas kernels  125 us (99%)
    pallas_call x1, Pallas kernels, local_step(): pl.pallas_call(functools.partial(exchange, chips), out_shape=(pltpu.VMEM(...  120 us
    pallas_call x1, Pallas kernels, local_step(): pl.pallas_call(place, out_shape=(out, out, out), in_specs=[vmem, vmem], o...  4.65 us

profile of v7, /device:TPU:113, one launch (start us, length us, event | category | flops | bytes accessed | tf_op | source)
XLA Modules:
  0.0 125.6 jit_solution(12283647961713890026)
XLA Ops:
  0.6 120.4 %shard_map.76 = (bf16[8192,256]{1,0:T(8,128)(2,1)S(1)}, bf16[2,8192,256]{2,1,0:T(8,128)(2,1)S(1)}) custom-call(bf16[1024,2304]{1,0:T(8,128)(2,1)} %x.1, f32[2304]{0:T(1024)} %gain.1, bf16[2304,256]{1,0:T(8,128)(2,1)} %bitcast.4, bf16[2304,128]{1,0:T(8,128)(2,1)} %wk.1, bf16[2304,128]{1,0:T(8,128)(2,1)} %wv.1), custom_call_target="tpu_custom_call" | custom-call | tf_op jit(solution)/shard_map/pallas_call | solution.py:299
  121.0 4.6 %shard_map.77 = (bf16[8192,256]{1,0:T(8,128)(2,1)}, bf16[8192,256]{1,0:T(8,128)(2,1)}, bf16[8192,256]{1,0:T(8,128)(2,1)}) custom-call(bf16[8192,256]{1,0:T(8,128)(2,1)S(1)} %get-tuple-element.8.oq, bf16[2,8192,256]{2,1,0:T(8,128)(2,1)S(1)} %get-tuple-element.9.okv), custom_call_target="tpu_custom_call" | custom-call | tf_op jit(solution)/shard_map/pallas_call | solution.py:326

commit v8 on v7

--- a/solution.py
+++ b/solution.py
@@ -12,7 +12,7 @@
 NORM_ROWS = 32
 CHUNK = 128
 OWN_ROWS = 256
-PLACE_BLOCKS = 2
+PLACE_BLOCKS = 1
 W_BLOCKS = 2
 W_FIRST = 256
 MESH = pl.DeviceIdType.MESH
@@ -71,12 +71,12 @@
         for peer in peers:
             pl.semaphore_signal(barrier, inc=1, device_id=peer, device_id_type=MESH)
 
-    greet((partner, weight_peer, weight_core(other_core)))
     follows = lax.div(2 * chip, chips) + half
     first = own_w_part(half, 0)
     first_src = wq.at[:, pl.ds(pl.multiple_of(half * LANES, LANES), LANES)]
     for r in range(W_BLOCKS):
         pltpu.make_async_copy(at_rows(first_src, 0, r), at_rows(first, 0, r), w0_sem.at[r]).start()
+    greet((partner, weight_peer, weight_core(other_core)))
     second = own_w_part(1 - half, 0)
     pltpu.make_async_copy(wq.at[:, pl.ds(pl.multiple_of((1 - half) * LANES, LANES), LANES)], second, wl_sem.at[0]).start()
     for h in range(2):
@@ -221,22 +221,10 @@
                 srq[1, c, at, lanes(h)] = both[:, :LANES]
                 srkv[1, h, at, lanes(c)] = both[:, LANES:]
         remote(srkv.at[1, :, at], okv.at[:, out], rkv_s, rkv_r.at[j], weight_peer).start()
-        for c in range(2):
+        for c in (1, 0):
             remote(srq.at[1, c, at], oq.at[out], rq_s, rq_r.at[core], weight_core(c)).start()
         local_products(1, near, start, CHUNK)
 
-    beside = pl.ds(block(core, weight_chip), rows)
-    arrived = okv.at[:, beside]
-    remote(arrived, arrived, okv_s, okv_r, weight_peer).wait_recv()
-    remote(arrived, arrived, fk_s.at[0], fk_r.at[0], partner).start()
-    far = block(core, far_chip)
-
-    @pl.loop(0, chunks)
-    def _(j):
-        piece = okv.at[:, pl.ds(pl.multiple_of(far + j * CHUNK, CHUNK), CHUNK)]
-        remote(piece, piece, rkv_s, rkv_r.at[j], weight_peer).wait_recv()
-        remote(piece, piece, fk_s.at[1], fk_r.at[1], partner).start()
-
     def all_q(c, on_chip):
         return oq.at[pl.ds(block(c, on_chip), rows)]
 
@@ -245,12 +233,9 @@
 
     for c in range(2):
         remote(all_q(c, weight_chip), all_q(c, weight_chip), oq_s, oq_r.at[c], weight_peer).wait_recv()
-        remote(all_q(c, far_chip), all_q(c, far_chip), rq_s, rq_r.at[c], weight_peer).wait_recv()
     for i, on_chip in enumerate((chip, token_chip)):
         remote(all_q(other_core, on_chip), all_q(other_core, on_chip), lq_s.at[i], lq_r.at[i], partner).wait_recv()
         remote(all_kv(other_core, on_chip), all_kv(other_core, on_chip), lkv_s.at[i], lkv_r.at[i], partner).wait_recv()
-    for i, on_chip in enumerate((weight_chip, far_chip)):
-        remote(all_kv(other_core, on_chip), all_kv(other_core, on_chip), fk_s.at[i], fk_r.at[i], partner).wait_recv()
 
     def sent(ref, sem):
         remote(ref, ref, sem, n_r.at[0], partner).wait_send()
@@ -262,12 +247,29 @@
         sent(w.at[1, 0, 0], wd_s.at[i])
         sent(slq.at[i], lq_s.at[i])
         sent(srkv.at[0], lkv_s.at[i])
-        sent(srkv.at[0], fk_s.at[i])
     sent(n.at[0], n_s)
     sent(srq.at[0], oq_s)
     sent(srkv.at[0], okv_s)
+
+    beside = pl.ds(block(core, weight_chip), rows)
+    arrived = okv.at[:, beside]
+    remote(arrived, arrived, okv_s, okv_r, weight_peer).wait_recv()
+    remote(arrived, arrived, fk_s.at[0], fk_r.at[0], partner).start()
+    far = block(core, far_chip)
+
+    @pl.loop(0, chunks)
+    def _(j):
+        piece = okv.at[:, pl.ds(pl.multiple_of(far + j * CHUNK, CHUNK), CHUNK)]
+        remote(piece, piece, rkv_s, rkv_r.at[j], weight_peer).wait_recv()
+        remote(piece, piece, fk_s.at[1], fk_r.at[1], partner).start()
+
+    sent(srkv.at[1], rkv_s)
+    for i, on_chip in enumerate((weight_chip, far_chip)):
+        sent(srkv.at[0], fk_s.at[i])
+        remote(all_kv(other_core, on_chip), all_kv(other_core, on_chip), fk_s.at[i], fk_r.at[i], partner).wait_recv()
     sent(srq.at[1], rq_s)
-    sent(srkv.at[1], rkv_s)
+    for c in range(2):
+        remote(all_q(c, far_chip), all_q(c, far_chip), rq_s, rq_r.at[c], weight_peer).wait_recv()
 
 
 def place(oq, okv, q, k, v, sems):

time: 126 us -> 125 us (level)
  no operation moved by 1% of the time
where the time goes in v8:
time: 125 us
  Pallas kernels  124 us (99%)
    pallas_call x1, Pallas kernels, local_step(): pl.pallas_call(functools.partial(exchange, chips), out_shape=(pltpu.VMEM(...  119 us
    pallas_call x1, Pallas kernels, local_step(): pl.pallas_call(place, out_shape=(out, out, out), in_specs=[vmem, vmem], o...  4.68 us

profile of v8, /device:TPU:113, one launch (start us, length us, event | category | flops | bytes accessed | tf_op | source)
XLA Modules:
  0.0 124.6 jit_solution(4425830181638503764)
XLA Ops:
  0.6 119.2 %shard_map.76 = (bf16[8192,256]{1,0:T(8,128)(2,1)S(1)}, bf16[2,8192,256]{2,1,0:T(8,128)(2,1)S(1)}) custom-call(bf16[1024,2304]{1,0:T(8,128)(2,1)} %x.1, f32[2304]{0:T(1024)} %gain.1, bf16[2304,256]{1,0:T(8,128)(2,1)} %bitcast.4, bf16[2304,128]{1,0:T(8,128)(2,1)} %wk.1, bf16[2304,128]{1,0:T(8,128)(2,1)} %wv.1), custom_call_target="tpu_custom_call" | custom-call | tf_op jit(solution)/shard_map/pallas_call | solution.py:301
  119.9 4.7 %shard_map.77 = (bf16[8192,256]{1,0:T(8,128)(2,1)}, bf16[8192,256]{1,0:T(8,128)(2,1)}, bf16[8192,256]{1,0:T(8,128)(2,1)}) custom-call(bf16[8192,256]{1,0:T(8,128)(2,1)S(1)} %get-tuple-element.8.oq, bf16[2,8192,256]{2,1,0:T(8,128)(2,1)S(1)} %get-tuple-element.9.okv), custom_call_target="tpu_custom_call" | custom-call | tf_op jit(solution)/shard_map/pallas_call | solution.py:328

commit v9 on v8

--- a/solution.py
+++ b/solution.py
@@ -12,7 +12,6 @@
 NORM_ROWS = 32
 CHUNK = 128
 OWN_ROWS = 256
-PLACE_BLOCKS = 1
 W_BLOCKS = 2
 W_FIRST = 256
 MESH = pl.DeviceIdType.MESH
@@ -270,19 +269,6 @@
     sent(srq.at[1], rq_s)
     for c in range(2):
         remote(all_q(c, far_chip), all_q(c, far_chip), rq_s, rq_r.at[c], weight_peer).wait_recv()
-
-
-def place(oq, okv, q, k, v, sems):
-    rows = oq.shape[0] // PLACE_BLOCKS
-    copies = []
-    for i in range(PLACE_BLOCKS):
-        at = pl.ds(i * rows, rows)
-        for a, (src, dst) in enumerate(((oq, q), (okv.at[0], k), (okv.at[1], v))):
-            copies.append(pltpu.make_async_copy(src.at[at], dst.at[at], sems.at[i, a]))
-    for copy in copies:
-        copy.start()
-    for copy in copies:
-        copy.wait()
 
 
 def solution(mesh):
@@ -324,15 +310,7 @@
             ],
             compiler_params=pltpu.CompilerParams(collective_id=0, has_side_effects=True, vmem_limit_bytes=46 * 1024 * 1024),
         )(x_rows, norm_gain, w_q.reshape(depth, head), w_k, w_v)
-        out = jax.ShapeDtypeStruct((tokens, head), dtype)
-        q, k, v = pl.pallas_call(
-            place,
-            out_shape=(out, out, out),
-            in_specs=[vmem, vmem],
-            out_specs=(any_space, any_space, any_space),
-            scratch_shapes=[dma((PLACE_BLOCKS, 3))],
-            compiler_params=pltpu.CompilerParams(vmem_limit_bytes=1024 * 1024),
-        )(pltpu.with_memory_space_constraint(oq, pltpu.VMEM), pltpu.with_memory_space_constraint(okv, pltpu.VMEM))
+        q, k, v = oq, okv[0], okv[1]
         return q[:, None, :], k[:, None, :], v[:, None, :]
 
     return jax.shard_map(local_step, mesh=mesh, in_specs=(P(("dp", "tp"), None), P(None), P(None, "tp", None), P(None, "tp"), P(None, "tp")), out_specs=(P("dp", "tp", None), P("dp", "tp", None), P("dp", "tp", None)), check_vma=False)

time: 125 us -> 126 us (level)
  local copies, waits for them, and re-layouts: 0 us -> 5.62 us
  Pallas kernels: 124 us -> 119 us
    pallas_call x1 -> x0, Pallas kernels: 4.68 us -> none  [local_step(): pl.pallas_call(place, out_shape=(out, out, out), in_specs=[vmem, vmem], o...]
    another operation x0 -> x1, local copies, waits for them, and re-layouts: none -> 3.6 us  [local_step(): return (q[:, None, :], k[:, None, :], v[:, None, :])]
    unnamed x0 -> x1, local copies, waits for them, and re-layouts: none -> 2.02 us
where the time goes in v9:
time: 126 us
  Pallas kernels  119 us (94%)
  local copies, waits for them, and re-layouts  5.62 us (4%)
    pallas_call x1, Pallas kernels, local_step(): pl.pallas_call(functools.partial(exchange, chips), out_shape=(pltpu.VMEM(...  119 us
    another operation x1, local copies, waits for them, and re-layouts, local_step(): return (q[:, None, :], k[:, None, :], v[:, None, :])  3.6 us

profile of v9, /device:TPU:113, one launch (start us, length us, event | category | flops | bytes accessed | tf_op | source)
XLA Modules:
  0.0 125.5 jit_solution(6603217545323168425)
XLA Ops:
  0.6 119.2 %shard_map.76 = (bf16[8192,256]{1,0:T(8,128)(2,1)S(1)}, bf16[2,8192,256]{2,1,0:T(8,128)(2,1)S(1)}) custom-call(bf16[1024,2304]{1,0:T(8,128)(2,1)} %x.1, f32[2304]{0:T(1024)} %gain.1, bf16[2304,256]{1,0:T(8,128)(2,1)} %bitcast.7, bf16[2304,128]{1,0:T(8,128)(2,1)} %wk.1, bf16[2304,128]{1,0:T(8,128)(2,1)} %wv.1), custom_call_target="tpu_custom_call" | custom-call | tf_op jit(solution)/shard_map/pallas_call | solution.py:287
  119.9 2.0 %copy.9 = bf16[8192,1,256]{2,0,1:T(8,128)(2,1)} copy(bf16[8192,1,256]{2,0,1:T(8,128)(2,1)S(1)} %bitcast.6) | data formatting | bytes 8388608
  121.9 3.6 %slice_bitcast_fusion = (bf16[8192,1,256]{2,0,1:T(8,128)(2,1)}, bf16[8192,1,256]{2,0,1:T(8,128)(2,1)}) fusion(bf16[2,8192,256]{2,1,0:T(8,128)(2,1)S(1)} %get-tuple-element.6), kind=kLoop, calls=%fused_computation | loop fusion | bytes 16777216 | tf_op jit(solution)/shard_map/broadcast_in_dim;squeeze | solution.py:314

commit v10 on v7

v10 whole, which is shorter than its diff:
```python
import functools

import jax
import jax.numpy as jnp
from jax import lax
from jax.experimental import pallas as pl
from jax.experimental.pallas import tpu as pltpu
from jax.sharding import PartitionSpec as P

EPSILON = 1e-6
LANES = 128
NORM_ROWS = 32
CHUNK = 128
EARLY = 4
EARLY_SENDS = 5
OWN_ROWS = 256
W_BLOCKS = 2
W_FIRST = 256
MESH = pl.DeviceIdType.MESH


class Place:
    def __init__(self, chips, rows):
        self.rows = rows
        group = lax.axis_index("dp")
        device = lax.axis_index("tp")
        self.half = lax.rem(group, 2)
        self.core = lax.rem(device, 2)
        self.chip = lax.div(device, 2)
        self.token_chip = chips - 1 - self.chip
        self.weight_chip = self.chip + 1 - 2 * lax.rem(self.chip, 2)
        self.far_chip = chips - 1 - self.weight_chip
        self.other_core = 1 - self.core
        self.partner = {"tp": 2 * self.chip + self.other_core}
        self.token_peer = {"tp": 2 * self.token_chip + self.core}
        self.weight_peer = self.weight_core(self.core)
        self.group_peer = {"dp": group + 1 - 2 * self.half}
        self.follows = lax.div(2 * self.chip, chips) + self.half
        self.sends = EARLY_SENDS + 2 * self.core

    def weight_core(self, c):
        return {"tp": 2 * self.weight_chip + c}

    def block(self, c, on_chip):
        return pl.multiple_of((2 * on_chip + c) * self.rows, self.rows)


def remote(src, dst, send, recv, to):
    return pltpu.make_async_remote_copy(src_ref=src, dst_ref=dst, send_sem=send, recv_sem=recv, device_id=to, device_id_type=MESH)


def arrive(ref, sem, frm):
    remote(ref, ref, sem, sem, frm).wait_recv()


def sent(ref, sem, to):
    remote(ref, ref, sem, sem, to).wait_send()


def lanes(i):
    return pl.ds(pl.multiple_of(i * LANES, LANES), LANES)


def chunk_of(j):
    return pl.ds(pl.multiple_of(j * CHUNK, CHUNK), CHUNK)


def greet(barrier, peers):
    for peer in peers:
        pl.semaphore_signal(barrier, inc=1, device_id=peer, device_id_type=MESH)


def product(n, w, blk, at, side, h, c):
    return jnp.dot(n[blk, at, :], w[side, h, c], preferred_element_type=jnp.float32).astype(jnp.bfloat16)


def local_products(me, n, w, oq, okv, slq, blk, base, start, size, stage, q_sems, kv_sems):
    at = pl.ds(start, size)
    out = pl.ds(pl.multiple_of(base + start, size), size)

    @pl.loop(0, 2)
    def _(h):
        for b in range(2):
            c = lax.rem(me.core + b, 2)
            both = product(n, w, blk, at, 0, h, c)
            if b == 0:
                oq[out, lanes(h)] = both[:, :LANES]
            else:
                slq[stage, lanes(h)] = both[:, :LANES]
            okv[h, out, lanes(c)] = both[:, LANES:]
    remote(slq.at[stage], oq.at[out], *q_sems, me.partner).start()
    remote(okv.at[:, out], okv.at[:, out], *kv_sems, me.partner).start()


def remote_products(n, w, at, srq, srkv, stage):
    @pl.loop(0, 2)
    def _(h):
        for c in range(2):
            both = product(n, w, 1, at, 1, h, c)
            srq[c, at, lanes(h)] = both[:, :LANES]
            srkv[h, stage, lanes(c)] = both[:, LANES:]


def early_products(me, n, w, oq, okv, srq, srkv, ek_s, ek_r, eq_s, eq_r):
    near = me.block(me.core, me.token_chip)

    @pl.loop(0, EARLY)
    def _(j):
        at = chunk_of(j)
        out = pl.ds(pl.multiple_of(near + j * CHUNK, CHUNK), CHUNK)
        remote_products(n, w, at, srq, srkv, at)
        remote(srkv.at[:, at], okv.at[:, out], ek_s, ek_r, me.weight_peer).start()
        remote(srq.at[me.core, at], oq.at[out], eq_s, eq_r, me.weight_peer).start()


def finish_early(me, oq, okv, srq, srkv, ek_s, ek_r, eq_s, eq_r):
    at = pl.ds(0, EARLY * CHUNK)
    out = pl.ds(me.block(me.core, me.far_chip), EARLY * CHUNK)
    sent(srkv.at[:, at], ek_s, me.weight_peer)
    sent(srq.at[me.core, at], eq_s, me.weight_peer)
    arrive(okv.at[:, out], ek_r, me.weight_peer)
    arrive(oq.at[out], eq_r, me.weight_peer)


def first_exchange(chips, x, gain, wq, wk, wv, oq, okv, n, w, srq, gain_copy, gain_row, slq, srq0, srkv0, srkv, g_sem, x_sem, w0_sem, wl_sem, wl_s, wl_r,
                   wx_s, wx_r, wg_s, wg_r, wd_s, wd_r, n_s, n_r, oq_s, oq_r, okv_s, okv_r, lq_s, lq_r, lkv_s, lkv_r, fk_s, fk_r, ek_s, ek_r, eq_s, eq_r):
    rows, depth = x.shape
    chunks = rows // CHUNK
    me = Place(chips, rows)
    half, core, other_core = me.half, me.core, me.other_core
    partner, token_peer, weight_peer, group_peer = me.partner, me.token_peer, me.weight_peer, me.group_peer
    weight_core, follows, sends = me.weight_core, me.follows, me.sends

    def load_x(j):
        return pltpu.make_async_copy(x.at[chunk_of(j)], n.at[0, chunk_of(j)], x_sem.at[j])

    q_half = [wq.at[:, pl.ds(h * LANES, LANES)] for h in range(2)]
    kv = [wk, wv]

    def own_w_part(h, part):
        return w.at[0, h, core, :, pl.ds(part * LANES, LANES)]

    cuts = ((0, W_FIRST, depth), (0, depth // 2, depth))

    def at_rows(ref, part, r):
        return ref.at[pl.ds(cuts[part][r], cuts[part][r + 1] - cuts[part][r])]

    barrier = pltpu.get_barrier_semaphore()

    first = own_w_part(half, 0)
    first_src = wq.at[:, pl.ds(pl.multiple_of(half * LANES, LANES), LANES)]
    for r in range(W_BLOCKS):
        pltpu.make_async_copy(at_rows(first_src, 0, r), at_rows(first, 0, r), w0_sem.at[r]).start()
    greet(barrier, (partner, weight_peer, weight_core(other_core)))
    second = own_w_part(1 - half, 0)
    pltpu.make_async_copy(wq.at[:, pl.ds(pl.multiple_of((1 - half) * LANES, LANES), LANES)], second, wl_sem.at[0]).start()
    for h in range(2):
        pltpu.make_async_copy(kv[h], own_w_part(h, 1), wl_sem.at[1 + h]).start()
    gain_load = pltpu.make_async_copy(gain, gain_copy, g_sem)
    gain_load.start()
    for j in range(chunks):
        load_x(j).start()
    pl.semaphore_wait(barrier, 3 + follows)
    greet(barrier, (token_peer, group_peer))

    w_parts = [w.at[1, half, core, :, pl.ds(part * LANES, LANES)] for part in range(2)]
    for r in range(W_BLOCKS):
        pltpu.make_async_copy(at_rows(first, 0, r), at_rows(first, 0, r), w0_sem.at[r]).wait()
        remote(at_rows(first, 0, r), at_rows(w_parts[0], 0, r), wx_s, wx_r.at[0, r], weight_peer).start()
    for h in range(2):
        @pl.when(half == h)
        def _():
            for r in range(W_BLOCKS):
                remote(at_rows(kv[h], 1, r), at_rows(w_parts[1], 1, r), wx_s, wx_r.at[1, r], weight_peer).start()
    for h in range(2):
        for part, src in enumerate((q_half[h], kv[h])):
            remote(src, own_w_part(h, part), wl_s, wl_r, partner).start()
    gain_load.wait()
    gain_row[...] = gain_copy[...].reshape(1, depth)

    def send_n(j):
        return remote(n.at[0, chunk_of(j)], n.at[1, chunk_of(j)], n_s, n_r.at[j], token_peer)

    @pl.loop(0, chunks)
    def _(j):
        load_x(j).wait()

        @pl.loop(0, CHUNK // NORM_ROWS)
        def _(i):
            at = pl.ds(pl.multiple_of(j * CHUNK + i * NORM_ROWS, NORM_ROWS), NORM_ROWS)
            wide = n[0, at, :].astype(jnp.float32)
            mean_sq = jnp.mean(wide * wide, axis=-1, keepdims=True)
            n[0, at, :] = (wide * lax.rsqrt(mean_sq + EPSILON) * gain_row[...]).astype(jnp.bfloat16)

        @pl.when(jnp.logical_and(j == 0, follows < 2))
        def _():
            pl.semaphore_wait(barrier, 2 - follows)

        @pl.when(j < sends)
        def _():
            send_n(j).start()

    own = me.block(core, me.chip)
    near = me.block(core, me.token_chip)

    def own_rows(start, size, stage):
        local_products(me, n, w, oq, okv, slq, 0, own, start, size, stage, (lq_s.at[0], lq_r.at[0]), (lkv_s.at[0], lkv_r.at[0]))

    own_w = w.at[0, :, core]
    pltpu.make_async_copy(second, second, wl_sem.at[0]).wait()
    for h in range(2):
        pltpu.make_async_copy(kv[h], own_w_part(h, 1), wl_sem.at[1 + h]).wait()
    other_w = w.at[0, :, other_core]
    remote(other_w, other_w, wl_s, wl_r, partner).wait_recv()

    def own_part(h, c, part):
        @pl.loop(0, rows // OWN_ROWS)
        def _(i):
            at = pl.ds(pl.multiple_of(i * OWN_ROWS, OWN_ROWS), OWN_ROWS)
            piece = w[1, h, c, :, part * LANES:(part + 1) * LANES]
            value = jnp.dot(n[0, at, :], piece, preferred_element_type=jnp.float32).astype(jnp.bfloat16)
            if part == 0:
                srq0[c, at, lanes(h)] = value
            else:
                srkv0[h, at, lanes(c)] = value

    def send_own(h, c, part):
        out = pl.ds(own, rows)
        if part == 0:
            remote(srq0.at[c, :, lanes(h)], oq.at[out, lanes(h)], oq_s, oq_r.at[core], weight_core(c)).start()
        else:
            remote(srkv0.at[h, :, lanes(c)], okv.at[h, out, lanes(c)], okv_s, okv_r, weight_peer).start()

    local_chunks = rows // OWN_ROWS
    steps = 2 * W_BLOCKS
    for step in range(steps):
        part, r = divmod(step, W_BLOCKS)
        piece = at_rows(w_parts[part], part, r)
        remote(piece, piece, wx_s, wx_r.at[part, r], weight_peer).wait_recv()
        remote(piece, piece, wg_s, wg_r, group_peer).start()
        remote(piece, piece, wd_s.at[0], wd_r.at[0], partner).start()
        if r == W_BLOCKS - 1:
            own_part(half, core, part)
            send_own(half, core, part)
        for i in range(step * local_chunks // steps, (step + 1) * local_chunks // steps):
            own_rows(i * OWN_ROWS, OWN_ROWS, pl.ds(i * OWN_ROWS, OWN_ROWS))

    def own_products(h, c):
        @pl.loop(0, rows // OWN_ROWS)
        def _(i):
            at = pl.ds(pl.multiple_of(i * OWN_ROWS, OWN_ROWS), OWN_ROWS)
            both = product(n, w, 0, at, 1, h, c)
            srq0[c, at, lanes(h)] = both[:, :LANES]
            srkv0[h, at, lanes(c)] = both[:, LANES:]
        for part in range(2):
            send_own(h, c, part)

    other_half = 1 - half
    from_partner = w.at[1, half, other_core]
    remote(from_partner, from_partner, wd_s.at[0], wd_r.at[0], partner).wait_recv()
    own_products(half, other_core)
    from_group = w.at[1, other_half, core]
    remote(from_group, from_group, wg_s, wg_r, group_peer).wait_recv()
    remote(from_group, from_group, wd_s.at[1], wd_r.at[1], partner).start()
    own_products(other_half, core)
    from_both = w.at[1, other_half, other_core]
    remote(from_both, from_both, wd_s.at[1], wd_r.at[1], partner).wait_recv()
    own_products(other_half, other_core)

    @pl.loop(0, EARLY)
    def _(j):
        send_n(j).wait_recv()
        start = pl.multiple_of(j * CHUNK, CHUNK)
        stage = pl.ds(pl.multiple_of(rows + start, CHUNK), CHUNK)
        local_products(me, n, w, oq, okv, slq, 1, near, start, CHUNK, stage, (lq_s.at[1], lq_r.at[1]), (lkv_s.at[1], lkv_r.at[1]))

    @pl.when(core == 1)
    def _():
        early_products(me, n, w, oq, okv, srq, srkv, ek_s, ek_r, eq_s, eq_r)

    @pl.loop(EARLY, sends)
    def _(j):
        send_n(j).wait_recv()

    for c in range(2):
        arrive(oq.at[pl.ds(me.block(c, me.weight_chip), rows)], oq_r.at[c], weight_peer)
    beside = okv.at[:, pl.ds(me.block(core, me.weight_chip), rows)]
    arrive(beside, okv_r, weight_peer)
    remote(beside, beside, fk_s, fk_r, partner).start()
    for i, (on_chip, size) in enumerate(((me.chip, rows), (me.token_chip, EARLY * CHUNK))):
        theirs = pl.ds(me.block(other_core, on_chip), size)
        mine = pl.ds(0, size)
        arrive(oq.at[theirs], lq_r.at[i], partner)
        arrive(okv.at[:, theirs], lkv_r.at[i], partner)
        sent(slq.at[mine], lq_s.at[i], partner)
        sent(okv.at[:, mine], lkv_s.at[i], partner)
    for i in range(2):
        @pl.when(core == i)
        def _():
            sent(n.at[0, pl.ds(0, (EARLY_SENDS + 2 * i) * CHUNK)], n_s, token_peer)
    sent(own_w, wl_s, partner)
    sent(w.at[1, 0, 0], wx_s, weight_peer)
    sent(w.at[1, 0, 0], wg_s, group_peer)
    for i in range(2):
        sent(w.at[1, 0, 0], wd_s.at[i], partner)
    sent(srq0, oq_s, weight_peer)
    sent(srkv0, okv_s, weight_peer)

    @pl.when(core == 1)
    def _():
        finish_early(me, oq, okv, srq, srkv, ek_s, ek_r, eq_s, eq_r)

    sent(beside, fk_s, partner)
    arrive(okv.at[:, pl.ds(me.block(other_core, me.weight_chip), rows)], fk_r, partner)


def second_exchange(chips, w, written, oq_in, okv_in, n_in, srq_in, oq, okv, n, srq, srkv, slq, n_s, n_r, ek_s, ek_r, eq_s, eq_r, xb_s, xb_r, rq_s, rq_r, rkv_s, rkv_r,
                    lq_s, lq_r, lkv_s, lkv_r, fe_s, fe_r, fk_s, fk_r):
    rows = n.shape[1]
    chunks = rows // CHUNK
    early = EARLY * CHUNK
    late = rows - early
    me = Place(chips, rows)
    core, other_core, partner, weight_peer = me.core, me.other_core, me.partner, me.weight_peer
    near = me.block(core, me.token_chip)
    far = me.block(core, me.far_chip)

    barrier = pltpu.get_barrier_semaphore()
    greet(barrier, (weight_peer, me.token_peer))
    pl.semaphore_wait(barrier, 2 + 2 * core)
    greet(barrier, (partner, me.weight_core(other_core)))

    def send_n(j):
        return remote(n.at[0, chunk_of(j)], n.at[1, chunk_of(j)], n_s, n_r.at[j], me.token_peer)

    @pl.loop(me.sends, chunks)
    def _(j):
        send_n(j).start()

    @pl.when(core == 0)
    def _():
        early_products(me, n, w, oq, okv, srq, srkv, ek_s, ek_r, eq_s, eq_r)
        pl.semaphore_wait(barrier, 2)

    remote(srq.at[other_core, pl.ds(0, early)], oq.at[pl.ds(near, early)], xb_s, xb_r, me.weight_core(other_core)).start()

    @pl.loop(EARLY, chunks)
    def _(j):
        @pl.when(j >= me.sends)
        def _():
            send_n(j).wait_recv()

        start = pl.multiple_of(j * CHUNK, CHUNK)
        at = pl.ds(start, CHUNK)
        out = pl.ds(pl.multiple_of(near + start, CHUNK), CHUNK)
        remote_products(n, w, at, srq, srkv, at)
        remote(srkv.at[:, at], okv.at[:, out], rkv_s, rkv_r.at[j - EARLY], weight_peer).start()
        for c in (1, 0):
            remote(srq.at[c, at], oq.at[out], rq_s, rq_r.at[core], me.weight_core(c)).start()
        stage = pl.ds(pl.multiple_of(start - early, CHUNK), CHUNK)
        local_products(me, n, w, oq, okv, slq, 1, near, start, CHUNK, stage, (lq_s, lq_r), (lkv_s, lkv_r))

    @pl.when(core == 0)
    def _():
        finish_early(me, oq, okv, srq, srkv, ek_s, ek_r, eq_s, eq_r)

    far_early = okv.at[:, pl.ds(far, early)]
    remote(far_early, far_early, fe_s, fe_r, partner).start()
    theirs = pl.ds(pl.multiple_of(me.block(other_core, me.token_chip) + early, CHUNK), late)
    arrive(oq.at[theirs], lq_r, partner)
    arrive(okv.at[:, theirs], lkv_r, partner)
    sent(slq, lq_s, partner)
    sent(okv.at[:, theirs], lkv_s, partner)
    arrive(oq.at[pl.ds(me.block(other_core, me.far_chip), early)], xb_r, weight_peer)
    sent(srq.at[other_core, pl.ds(0, early)], xb_s, weight_peer)
    for i in range(2):
        @pl.when(core == i)
        def _():
            sent(n.at[0, pl.ds((EARLY_SENDS + 2 * i) * CHUNK, rows - (EARLY_SENDS + 2 * i) * CHUNK)], n_s, me.token_peer)

    @pl.loop(EARLY, chunks)
    def _(j):
        piece = okv.at[:, pl.ds(pl.multiple_of(far + j * CHUNK, CHUNK), CHUNK)]
        remote(piece, piece, rkv_s, rkv_r.at[j - EARLY], weight_peer).wait_recv()
        remote(piece, piece, fk_s, fk_r, partner).start()

    tail = pl.ds(early, late)
    sent(srkv.at[:, tail], rkv_s, weight_peer)
    sent(far_early, fe_s, partner)
    sent(srkv.at[:, tail], fk_s, partner)
    arrive(okv.at[:, pl.ds(me.block(other_core, me.far_chip), early)], fe_r, partner)
    arrive(okv.at[:, pl.ds(pl.multiple_of(me.block(other_core, me.far_chip) + early, CHUNK), late)], fk_r, partner)
    sent(srq.at[:, tail], rq_s, weight_peer)
    for c in range(2):
        arrive(oq.at[pl.ds(pl.multiple_of(me.block(c, me.far_chip) + early, CHUNK), late)], rq_r.at[c], weight_peer)


def write_rows(blocks, oq, okv, q, k, v, sems):
    copies = []
    for i, (start, size) in enumerate(blocks):
        at = pl.ds(start, size)
        for a, (src, dst) in enumerate(((oq, q), (okv.at[0], k), (okv.at[1], v))):
            copies.append(pltpu.make_async_copy(src.at[at], dst.at[at], sems.at[i, a]))
    for copy in copies:
        copy.start()
    for copy in copies:
        copy.wait()


def first_write(chips, rows, oq, okv, q, k, v, written, sems):
    me = Place(chips, rows)
    written[...] = jnp.zeros_like(written)
    blocks = [(me.block(0, me.chip), 2 * rows), (me.block(0, me.weight_chip), 2 * rows)]
    blocks += [(me.block(c, me.token_chip), EARLY * CHUNK) for c in range(2)]
    write_rows(blocks, oq, okv, q, k, v, sems)


def last_write(chips, rows, oq, okv, q_in, k_in, v_in, q, k, v, sems):
    me = Place(chips, rows)
    early = EARLY * CHUNK
    blocks = [(me.block(0, me.far_chip), 2 * rows)]
    blocks += [(pl.multiple_of(me.block(c, me.token_chip) + early, CHUNK), rows - early) for c in range(2)]
    write_rows(blocks, oq, okv, q, k, v, sems)


def solution(mesh):
    group_size = mesh.shape["tp"]
    chips = group_size // 2

    def local_step(x_rows, norm_gain, w_q, w_k, w_v):
        rows, depth = x_rows.shape
        head = w_q.shape[2]
        tokens = rows * group_size
        dtype = x_rows.dtype
        any_space = pl.BlockSpec(memory_space=pl.ANY)
        vmem = pl.BlockSpec(memory_space=pltpu.VMEM)
        dma = pltpu.SemaphoreType.DMA
        chunks = rows // CHUNK
        early = EARLY * CHUNK
        oq_type, okv_type = pltpu.VMEM((tokens, head), dtype), pltpu.VMEM((2, tokens, head), dtype)
        n_type, srq_type = pltpu.VMEM((2, rows, depth), dtype), pltpu.VMEM((2, rows, head), dtype)

        def held(*arrays):
            return [pltpu.with_memory_space_constraint(a, pltpu.VMEM) for a in arrays]

        oq, okv, n, w, srq = pl.pallas_call(
            functools.partial(first_exchange, chips),
            out_shape=(oq_type, okv_type, n_type, pltpu.VMEM((2, 2, 2, depth, 2 * LANES), dtype), srq_type),
            in_specs=[any_space] * 5,
            out_specs=(vmem,) * 5,
            scratch_shapes=[
                pltpu.VMEM((depth,), norm_gain.dtype),
                pltpu.VMEM((1, depth), norm_gain.dtype),
                pltpu.VMEM((rows + early, head), dtype),
                pltpu.VMEM((2, rows, head), dtype),
                pltpu.VMEM((2, rows, head), dtype),
                pltpu.VMEM((2, early, head), dtype),
                dma, dma((chunks,)),
                dma((W_BLOCKS,)), dma((3,)), dma, dma,
                dma, dma((2, W_BLOCKS)),
                dma, dma,
                dma((2,)), dma((2,)),
                dma, dma((chunks,)),
                dma, dma((2,)), dma, dma,
                dma((2,)), dma((2,)), dma((2,)), dma((2,)),
                dma, dma, dma, dma, dma, dma,
            ],
            compiler_params=pltpu.CompilerParams(collective_id=0, has_side_effects=True, vmem_limit_bytes=16 * 1024 * 1024),
        )(*[pltpu.with_memory_space_constraint(a, pltpu.HBM) for a in (x_rows, norm_gain, w_q.reshape(depth, head), w_k, w_v)])
        out = jax.ShapeDtypeStruct((tokens, head), dtype)
        q, k, v, written = pl.pallas_call(
            functools.partial(first_write, chips, rows),
            out_shape=(out, out, out, jax.ShapeDtypeStruct((8, LANES), jnp.float32)),
            in_specs=[vmem, vmem],
            out_specs=(any_space, any_space, any_space, vmem),
            scratch_shapes=[dma((4, 3))],
            compiler_params=pltpu.CompilerParams(vmem_limit_bytes=1024 * 1024),
        )(*held(oq, okv))
        oq, okv, _, _ = pl.pallas_call(
            functools.partial(second_exchange, chips),
            out_shape=(oq_type, okv_type, n_type, srq_type),
            in_specs=[vmem, any_space, vmem, vmem, vmem, vmem],
            out_specs=(vmem,) * 4,
            input_output_aliases={2: 0, 3: 1, 4: 2, 5: 3},
            scratch_shapes=[
                pltpu.VMEM((2, rows, head), dtype),
                pltpu.VMEM((rows - early, head), dtype),
                dma, dma((chunks,)),
                dma, dma, dma, dma, dma, dma,
                dma, dma((2,)), dma, dma((chunks - EARLY,)),
                dma, dma, dma, dma,
                dma, dma, dma, dma,
            ],
            compiler_params=pltpu.CompilerParams(collective_id=1, has_side_effects=True, vmem_limit_bytes=16 * 1024 * 1024),
        )(*held(w), written, *held(oq, okv, n, srq))
        q, k, v = pl.pallas_call(
            functools.partial(last_write, chips, rows),
            out_shape=(out, out, out),
            in_specs=[vmem, vmem, any_space, any_space, any_space],
            out_specs=(any_space, any_space, any_space),
            input_output_aliases={2: 0, 3: 1, 4: 2},
            scratch_shapes=[dma((3, 3))],
            compiler_params=pltpu.CompilerParams(vmem_limit_bytes=1024 * 1024),
        )(*held(oq, okv), q, k, v)
        return q[:, None, :], k[:, None, :], v[:, None, :]

    return jax.shard_map(local_step, mesh=mesh, in_specs=(P(("dp", "tp"), None), P(None), P(None, "tp", None), P(None, "tp"), P(None, "tp")), out_specs=(P("dp", "tp", None), P("dp", "tp", None), P("dp", "tp", None)), check_vma=False)
```

time: 126 us -> 134 us (1.063)
  Pallas kernels: 125 us -> 133 us
    pallas_call x2 -> x4, Pallas kernels: 125 us -> 133 us  [the longest x1 86.8 us: local_step(): pl.pallas_call(functools.partial(first_exchange, chips), out_shape=(oq_ty...]
where the time goes in v10:
time: 134 us
  Pallas kernels  133 us (99%)
    pallas_call x1, Pallas kernels, local_step(): pl.pallas_call(functools.partial(first_exchange, chips), out_shape=(oq_ty...  86.8 us
    pallas_call x1, Pallas kernels, local_step(): pl.pallas_call(functools.partial(second_exchange, chips), out_shape=(oq_t...  40.8 us
    pallas_call x1, Pallas kernels, local_step(): pl.pallas_call(functools.partial(first_write, chips, rows), out_shape=(ou...  3.22 us

profile of v10, /device:TPU:113, one launch (start us, length us, event | category | flops | bytes accessed | tf_op | source)
XLA Modules:
  0.0 133.7 jit_solution(9246722163990441964)
XLA Ops:
  0.6 86.8 %shard_map.76 = (bf16[8192,256]{1,0:T(8,128)(2,1)S(1)}, bf16[2,8192,256]{2,1,0:T(8,128)(2,1)S(1)}, bf16[2,1024,2304]{2,1,0:T(8,128)(2,1)S(1)}, bf16[2,2,2,2304,2...) custom-call(bf16[1024,2304]{1,0:T(8,128)(2,1)} %x.1, f32[2304]{0:T(1024)} %gain.1, bf16[2304,256]{1,0:T(8,128)(2,1)} %bitcast.7, ...), custom_call_target="tpu_custom_call" | custom-call | tf_op jit(solution)/shard_map/pallas_call | solution.py:446
  87.5 3.2 %shard_map.77 = (bf16[8192,256]{1,0:T(8,128)(2,1)}, bf16[8192,256]{1,0:T(8,128)(2,1)}, bf16[8192,256]{1,0:T(8,128)(2,1)}, f32[8,128]{1,0:T(8,128)S(1)}) custom-call(bf16[8192,256]{1,0:T(8,128)(2,1)S(1)} %get-tuple-element.18.oq.oq_in, bf16[2,8192,256]{2,1,0:T(8,128)(2,1)S(1)} %get-tuple-element.19.okv.okv_in), custom_call_target="tpu_custom_call" | custom-call | tf_op jit(solution)/shard_map/pallas_call | solution.py:471
  90.7 40.8 %shard_map.78 = (bf16[8192,256]{1,0:T(8,128)(2,1)S(1)}, bf16[2,8192,256]{2,1,0:T(8,128)(2,1)S(1)}, bf16[2,1024,2304]{2,1,0:T(8,128)(2,1)S(1)}, bf16[2,1024,256]{2,1,0:T(8,128)(2,1)S(1)}) custom-call(bf16[2,2,2,2304,256]{4,3,2,1,0:T(8,128)(2,1)S(1)} %get-tuple-element.17.w, ...), custom_call_target="tpu_custom_call", output_to_operand_aliasing={{0}: (2, {}), {1}: (3, {}), {2}: (4, {}), {3}: (5, {})} | custom-call | tf_op jit(solution)/shard_map/pallas_call | solution.py:479
  131.5 2.3 %shard_map.79 = (bf16[8192,256]{1,0:T(8,128)(2,1)}, bf16[8192,256]{1,0:T(8,128)(2,1)}, bf16[8192,256]{1,0:T(8,128)(2,1)}) custom-call(bf16[8192,256]{1,0:T(8,128)(2,1)S(1)} %get-tuple-element.23.oq, bf16[2,8192,256]{2,1,0:T(8,128)(2,1)S(1)} %get-tuple-element.24.okv, ...), custom_call_target="tpu_custom_call", output_to_operand_aliasing={{0}: (2, {}), {1}: (3, {}), {2}: (4, {})} | custom-call | tf_op jit(solution)/shard_map/pallas_call | solution.py:496

commit v11 on v10

--- a/solution.py
+++ b/solution.py
@@ -278,10 +278,6 @@
     def _():
         early_products(me, n, w, oq, okv, srq, srkv, ek_s, ek_r, eq_s, eq_r)
 
-    @pl.loop(EARLY, sends)
-    def _(j):
-        send_n(j).wait_recv()
-
     for c in range(2):
         arrive(oq.at[pl.ds(me.block(c, me.weight_chip), rows)], oq_r.at[c], weight_peer)
     beside = okv.at[:, pl.ds(me.block(core, me.weight_chip), rows)]
@@ -294,6 +290,10 @@
         arrive(okv.at[:, theirs], lkv_r.at[i], partner)
         sent(slq.at[mine], lq_s.at[i], partner)
         sent(okv.at[:, mine], lkv_s.at[i], partner)
+    @pl.loop(EARLY, sends)
+    def _(j):
+        send_n(j).wait_recv()
+
     for i in range(2):
         @pl.when(core == i)
         def _():

time: 134 us -> 127 us (0.948)
  Pallas kernels: 133 us -> 127 us
    pallas_call x1, Pallas kernels: 40.8 us -> 36.6 us  [local_step(): pl.pallas_call(functools.partial(second_exchange, chips), out_shape=(oq_t...]
    pallas_call x1, Pallas kernels: 86.8 us -> 84.6 us  [local_step(): pl.pallas_call(functools.partial(first_exchange, chips), out_shape=(oq_ty...]
where the time goes in v11:
time: 127 us
  Pallas kernels  127 us (100%)
    pallas_call x1, Pallas kernels, local_step(): pl.pallas_call(functools.partial(first_exchange, chips), out_shape=(oq_ty...  84.6 us
    pallas_call x1, Pallas kernels, local_step(): pl.pallas_call(functools.partial(second_exchange, chips), out_shape=(oq_t...  36.6 us
    pallas_call x1, Pallas kernels, local_step(): pl.pallas_call(functools.partial(first_write, chips, rows), out_shape=(ou...  3.22 us

profile of v11, /device:TPU:113, one launch (start us, length us, event | category | flops | bytes accessed | tf_op | source)
XLA Modules:
  0.0 127.3 jit_solution(6322104493303860187)
XLA Ops:
  0.6 84.6 %shard_map.76 = (bf16[8192,256]{1,0:T(8,128)(2,1)S(1)}, bf16[2,8192,256]{2,1,0:T(8,128)(2,1)S(1)}, bf16[2,1024,2304]{2,1,0:T(8,128)(2,1)S(1)}, bf16[2,2,2,2304,2...) custom-call(bf16[1024,2304]{1,0:T(8,128)(2,1)} %x.1, f32[2304]{0:T(1024)} %gain.1, bf16[2304,256]{1,0:T(8,128)(2,1)} %bitcast.7, ...), custom_call_target="tpu_custom_call" | custom-call | tf_op jit(solution)/shard_map/pallas_call | solution.py:446
  85.2 3.2 %shard_map.77 = (bf16[8192,256]{1,0:T(8,128)(2,1)}, bf16[8192,256]{1,0:T(8,128)(2,1)}, bf16[8192,256]{1,0:T(8,128)(2,1)}, f32[8,128]{1,0:T(8,128)S(1)}) custom-call(bf16[8192,256]{1,0:T(8,128)(2,1)S(1)} %get-tuple-element.18.oq.oq_in, bf16[2,8192,256]{2,1,0:T(8,128)(2,1)S(1)} %get-tuple-element.19.okv.okv_in), custom_call_target="tpu_custom_call" | custom-call | tf_op jit(solution)/shard_map/pallas_call | solution.py:471
  88.4 36.6 %shard_map.78 = (bf16[8192,256]{1,0:T(8,128)(2,1)S(1)}, bf16[2,8192,256]{2,1,0:T(8,128)(2,1)S(1)}, bf16[2,1024,2304]{2,1,0:T(8,128)(2,1)S(1)}, bf16[2,1024,256]{2,1,0:T(8,128)(2,1)S(1)}) custom-call(bf16[2,2,2,2304,256]{4,3,2,1,0:T(8,128)(2,1)S(1)} %get-tuple-element.17.w, ...), custom_call_target="tpu_custom_call", output_to_operand_aliasing={{0}: (2, {}), {1}: (3, {}), {2}: (4, {}), {3}: (5, {})} | custom-call | tf_op jit(solution)/shard_map/pallas_call | solution.py:479
  125.0 2.3 %shard_map.79 = (bf16[8192,256]{1,0:T(8,128)(2,1)}, bf16[8192,256]{1,0:T(8,128)(2,1)}, bf16[8192,256]{1,0:T(8,128)(2,1)}) custom-call(bf16[8192,256]{1,0:T(8,128)(2,1)S(1)} %get-tuple-element.23.oq, bf16[2,8192,256]{2,1,0:T(8,128)(2,1)S(1)} %get-tuple-element.24.okv, ...), custom_call_target="tpu_custom_call", output_to_operand_aliasing={{0}: (2, {}), {1}: (3, {}), {2}: (4, {})} | custom-call | tf_op jit(solution)/shard_map/pallas_call | solution.py:496

commit v12 on v11

--- a/solution.py
+++ b/solution.py
@@ -11,7 +11,7 @@
 LANES = 128
 NORM_ROWS = 32
 CHUNK = 128
-EARLY = 4
+EARLY = 5
 EARLY_SENDS = 5
 OWN_ROWS = 256
 W_BLOCKS = 2
@@ -101,16 +101,10 @@
             srkv[h, stage, lanes(c)] = both[:, LANES:]
 
 
-def early_products(me, n, w, oq, okv, srq, srkv, ek_s, ek_r, eq_s, eq_r):
-    near = me.block(me.core, me.token_chip)
-
-    @pl.loop(0, EARLY)
-    def _(j):
-        at = chunk_of(j)
-        out = pl.ds(pl.multiple_of(near + j * CHUNK, CHUNK), CHUNK)
-        remote_products(n, w, at, srq, srkv, at)
-        remote(srkv.at[:, at], okv.at[:, out], ek_s, ek_r, me.weight_peer).start()
-        remote(srq.at[me.core, at], oq.at[out], eq_s, eq_r, me.weight_peer).start()
+def send_early(me, at, oq, okv, srq, srkv, ek_s, ek_r, eq_s, eq_r):
+    out = pl.ds(pl.multiple_of(me.block(me.core, me.token_chip) + at.start, CHUNK), at.size)
+    remote(srkv.at[:, at], okv.at[:, out], ek_s, ek_r, me.weight_peer).start()
+    remote(srq.at[me.core, at], oq.at[out], eq_s, eq_r, me.weight_peer).start()
 
 
 def finish_early(me, oq, okv, srq, srkv, ek_s, ek_r, eq_s, eq_r):
@@ -122,7 +116,7 @@
     arrive(oq.at[out], eq_r, me.weight_peer)
 
 
-def first_exchange(chips, x, gain, wq, wk, wv, oq, okv, n, w, srq, gain_copy, gain_row, slq, srq0, srkv0, srkv, g_sem, x_sem, w0_sem, wl_sem, wl_s, wl_r,
+def first_exchange(chips, x, gain, wq, wk, wv, oq, okv, n, w, srq, srkv, gain_copy, gain_row, slq, srq0, srkv0, g_sem, x_sem, w0_sem, wl_sem, wl_s, wl_r,
                    wx_s, wx_r, wg_s, wg_r, wd_s, wd_r, n_s, n_r, oq_s, oq_r, okv_s, okv_r, lq_s, lq_r, lkv_s, lkv_r, fk_s, fk_r, ek_s, ek_r, eq_s, eq_r):
     rows, depth = x.shape
     chunks = rows // CHUNK
@@ -272,11 +266,14 @@
         send_n(j).wait_recv()
         start = pl.multiple_of(j * CHUNK, CHUNK)
         stage = pl.ds(pl.multiple_of(rows + start, CHUNK), CHUNK)
+        at = chunk_of(j)
+        remote_products(n, w, at, srq, srkv, at)
+
+        @pl.when(core == 1)
+        def _():
+            send_early(me, at, oq, okv, srq, srkv, ek_s, ek_r, eq_s, eq_r)
+
         local_products(me, n, w, oq, okv, slq, 1, near, start, CHUNK, stage, (lq_s.at[1], lq_r.at[1]), (lkv_s.at[1], lkv_r.at[1]))
-
-    @pl.when(core == 1)
-    def _():
-        early_products(me, n, w, oq, okv, srq, srkv, ek_s, ek_r, eq_s, eq_r)
 
     for c in range(2):
         arrive(oq.at[pl.ds(me.block(c, me.weight_chip), rows)], oq_r.at[c], weight_peer)
@@ -314,7 +311,7 @@
     arrive(okv.at[:, pl.ds(me.block(other_core, me.weight_chip), rows)], fk_r, partner)
 
 
-def second_exchange(chips, w, written, oq_in, okv_in, n_in, srq_in, oq, okv, n, srq, srkv, slq, n_s, n_r, ek_s, ek_r, eq_s, eq_r, xb_s, xb_r, rq_s, rq_r, rkv_s, rkv_r,
+def second_exchange(chips, w, srkv_early, written, oq_in, okv_in, n_in, srq_in, oq, okv, n, srq, srkv, slq, n_s, n_r, ek_s, ek_r, eq_s, eq_r, xb_s, xb_r, rq_s, rq_r, rkv_s, rkv_r,
                     lq_s, lq_r, lkv_s, lkv_r, fe_s, fe_r, fk_s, fk_r):
     rows = n.shape[1]
     chunks = rows // CHUNK
@@ -339,7 +336,7 @@
 
     @pl.when(core == 0)
     def _():
-        early_products(me, n, w, oq, okv, srq, srkv, ek_s, ek_r, eq_s, eq_r)
+        send_early(me, pl.ds(0, early), oq, okv, srq, srkv_early, ek_s, ek_r, eq_s, eq_r)
         pl.semaphore_wait(barrier, 2)
 
     remote(srq.at[other_core, pl.ds(0, early)], oq.at[pl.ds(near, early)], xb_s, xb_r, me.weight_core(other_core)).start()
@@ -362,7 +359,7 @@
 
     @pl.when(core == 0)
     def _():
-        finish_early(me, oq, okv, srq, srkv, ek_s, ek_r, eq_s, eq_r)
+        finish_early(me, oq, okv, srq, srkv_early, ek_s, ek_r, eq_s, eq_r)
 
     far_early = okv.at[:, pl.ds(far, early)]
     remote(far_early, far_early, fe_s, fe_r, partner).start()
@@ -443,18 +440,17 @@
         def held(*arrays):
             return [pltpu.with_memory_space_constraint(a, pltpu.VMEM) for a in arrays]
 
-        oq, okv, n, w, srq = pl.pallas_call(
+        oq, okv, n, w, srq, srkv = pl.pallas_call(
             functools.partial(first_exchange, chips),
-            out_shape=(oq_type, okv_type, n_type, pltpu.VMEM((2, 2, 2, depth, 2 * LANES), dtype), srq_type),
+            out_shape=(oq_type, okv_type, n_type, pltpu.VMEM((2, 2, 2, depth, 2 * LANES), dtype), srq_type, pltpu.VMEM((2, early, head), dtype)),
             in_specs=[any_space] * 5,
-            out_specs=(vmem,) * 5,
+            out_specs=(vmem,) * 6,
             scratch_shapes=[
                 pltpu.VMEM((depth,), norm_gain.dtype),
                 pltpu.VMEM((1, depth), norm_gain.dtype),
                 pltpu.VMEM((rows + early, head), dtype),
                 pltpu.VMEM((2, rows, head), dtype),
                 pltpu.VMEM((2, rows, head), dtype),
-                pltpu.VMEM((2, early, head), dtype),
                 dma, dma((chunks,)),
                 dma((W_BLOCKS,)), dma((3,)), dma, dma,
                 dma, dma((2, W_BLOCKS)),
@@ -479,9 +475,9 @@
         oq, okv, _, _ = pl.pallas_call(
             functools.partial(second_exchange, chips),
             out_shape=(oq_type, okv_type, n_type, srq_type),
-            in_specs=[vmem, any_space, vmem, vmem, vmem, vmem],
+            in_specs=[vmem, vmem, any_space, vmem, vmem, vmem, vmem],
             out_specs=(vmem,) * 4,
-            input_output_aliases={2: 0, 3: 1, 4: 2, 5: 3},
+            input_output_aliases={3: 0, 4: 1, 5: 2, 6: 3},
             scratch_shapes=[
                 pltpu.VMEM((2, rows, head), dtype),
                 pltpu.VMEM((rows - early, head), dtype),
@@ -492,7 +488,7 @@
                 dma, dma, dma, dma,
             ],
             compiler_params=pltpu.CompilerParams(collective_id=1, has_side_effects=True, vmem_limit_bytes=16 * 1024 * 1024),
-        )(*held(w), written, *held(oq, okv, n, srq))
+        )(*held(w, srkv), written, *held(oq, okv, n, srq))
         q, k, v = pl.pallas_call(
             functools.partial(last_write, chips, rows),
             out_shape=(out, out, out),

time: 127 us -> 124 us (0.976)
  Pallas kernels: 127 us -> 124 us
    pallas_call x1, Pallas kernels: 36.6 us -> 32.8 us  [local_step(): pl.pallas_call(functools.partial(second_exchange, chips), out_shape=(oq_t...]
where the time goes in v12:
time: 124 us
  Pallas kernels  124 us (100%)
    pallas_call x1, Pallas kernels, local_step(): pl.pallas_call(functools.partial(first_exchange, chips), out_shape=(oq_ty...  85.2 us
    pallas_call x1, Pallas kernels, local_step(): pl.pallas_call(functools.partial(second_exchange, chips), out_shape=(oq_t...  32.8 us
    pallas_call x1, Pallas kernels, local_step(): pl.pallas_call(functools.partial(first_write, chips, rows), out_shape=(ou...  3.34 us

profile of v12, /device:TPU:113, one launch (start us, length us, event | category | flops | bytes accessed | tf_op | source)
XLA Modules:
  0.0 124.2 jit_solution(18134609634782343051)
XLA Ops:
  0.6 85.2 %shard_map.76 = (bf16[8192,256]{1,0:T(8,128)(2,1)S(1)}, bf16[2,8192,256]{2,1,0:T(8,128)(2,1)S(1)}, bf16[2,1024,2304]{2,1,0:T(8,128)(2,1)S(1)}, bf16[2,2,2,2304,2...) custom-call(bf16[1024,2304]{1,0:T(8,128)(2,1)} %x.1, f32[2304]{0:T(1024)} %gain.1, ...), custom_call_target="tpu_custom_call" | custom-call | tf_op jit(solution)/shard_map/pallas_call | solution.py:443
  85.9 3.3 %shard_map.77 = (bf16[8192,256]{1,0:T(8,128)(2,1)}, bf16[8192,256]{1,0:T(8,128)(2,1)}, bf16[8192,256]{1,0:T(8,128)(2,1)}, f32[8,128]{1,0:T(8,128)S(1)}) custom-call(bf16[8192,256]{1,0:T(8,128)(2,1)S(1)} %get-tuple-element.20.oq.oq_in, bf16[2,8192,256]{2,1,0:T(8,128)(2,1)S(1)} %get-tuple-element.21.okv.okv_in), custom_call_target="tpu_custom_call" | custom-call | tf_op jit(solution)/shard_map/pallas_call | solution.py:467
  89.2 32.8 %shard_map.78 = (bf16[8192,256]{1,0:T(8,128)(2,1)S(1)}, bf16[2,8192,256]{2,1,0:T(8,128)(2,1)S(1)}, bf16[2,1024,2304]{2,1,0:T(8,128)(2,1)S(1)}, bf16[2,1024,256]{2,1,0:T(8,128)(2,1)S(1)}) custom-call(bf16[2,2,2,2304,256]{4,3,2,1,0:T(8,128)(2,1)S(1)} %get-tuple-element.18.w, ...), custom_call_target="tpu_custom_call", output_to_operand_aliasing={{0}: (3, {}), {1}: (4, {}), {2}: (5, {}), {3}: (6, {})} | custom-call | tf_op jit(solution)/shard_map/pallas_call | solution.py:475
  122.0 2.1 %shard_map.79 = (bf16[8192,256]{1,0:T(8,128)(2,1)}, bf16[8192,256]{1,0:T(8,128)(2,1)}, bf16[8192,256]{1,0:T(8,128)(2,1)}) custom-call(bf16[8192,256]{1,0:T(8,128)(2,1)S(1)} %get-tuple-element.25.oq, bf16[2,8192,256]{2,1,0:T(8,128)(2,1)S(1)} %get-tuple-element.26.okv, ...), custom_call_target="tpu_custom_call", output_to_operand_aliasing={{0}: (2, {}), {1}: (3, {}), {2}: (4, {})} | custom-call | tf_op jit(solution)/shard_map/pallas_call | solution.py:492

commit v13 on v12

--- a/solution.py
+++ b/solution.py
@@ -13,6 +13,7 @@
 CHUNK = 128
 EARLY = 5
 EARLY_SENDS = 5
+MORE_SENDS = 3
 OWN_ROWS = 256
 W_BLOCKS = 2
 W_FIRST = 256
@@ -36,7 +37,7 @@
         self.weight_peer = self.weight_core(self.core)
         self.group_peer = {"dp": group + 1 - 2 * self.half}
         self.follows = lax.div(2 * self.chip, chips) + self.half
-        self.sends = EARLY_SENDS + 2 * self.core
+        self.sends = EARLY_SENDS + MORE_SENDS * self.core
 
     def weight_core(self, c):
         return {"tp": 2 * self.weight_chip + c}
@@ -294,7 +295,7 @@
     for i in range(2):
         @pl.when(core == i)
         def _():
-            sent(n.at[0, pl.ds(0, (EARLY_SENDS + 2 * i) * CHUNK)], n_s, token_peer)
+            sent(n.at[0, pl.ds(0, (EARLY_SENDS + MORE_SENDS * i) * CHUNK)], n_s, token_peer)
     sent(own_w, wl_s, partner)
     sent(w.at[1, 0, 0], wx_s, weight_peer)
     sent(w.at[1, 0, 0], wg_s, group_peer)
@@ -371,9 +372,11 @@
     arrive(oq.at[pl.ds(me.block(other_core, me.far_chip), early)], xb_r, weight_peer)
     sent(srq.at[other_core, pl.ds(0, early)], xb_s, weight_peer)
     for i in range(2):
-        @pl.when(core == i)
-        def _():
-            sent(n.at[0, pl.ds((EARLY_SENDS + 2 * i) * CHUNK, rows - (EARLY_SENDS + 2 * i) * CHUNK)], n_s, me.token_peer)
+        gone = (EARLY_SENDS + MORE_SENDS * i) * CHUNK
+        if gone < rows:
+            @pl.when(core == i)
+            def _():
+                sent(n.at[0, pl.ds(gone, rows - gone)], n_s, me.token_peer)
 
     @pl.loop(EARLY, chunks)
     def _(j):

time: 124 us -> 127 us (1.024)
  Pallas kernels: 124 us -> 126 us
    pallas_call x1, Pallas kernels: 85.2 us -> 94.4 us  [local_step(): pl.pallas_call(functools.partial(first_exchange, chips), out_shape=(oq_ty...]
    pallas_call x1, Pallas kernels: 32.8 us -> 26.3 us  [local_step(): pl.pallas_call(functools.partial(second_exchange, chips), out_shape=(oq_t...]
where the time goes in v13:
time: 127 us
  Pallas kernels  126 us (99%)
    pallas_call x1, Pallas kernels, local_step(): pl.pallas_call(functools.partial(first_exchange, chips), out_shape=(oq_ty...  94.4 us
    pallas_call x1, Pallas kernels, local_step(): pl.pallas_call(functools.partial(second_exchange, chips), out_shape=(oq_t...  26.3 us
    pallas_call x1, Pallas kernels, local_step(): pl.pallas_call(functools.partial(first_write, chips, rows), out_shape=(ou...  3.34 us

profile of v13, /device:TPU:113, one launch (start us, length us, event | category | flops | bytes accessed | tf_op | source)
XLA Modules:
  0.0 126.8 jit_solution(7570082124584008400)
XLA Ops:
  0.6 94.4 %shard_map.76 = (bf16[8192,256]{1,0:T(8,128)(2,1)S(1)}, bf16[2,8192,256]{2,1,0:T(8,128)(2,1)S(1)}, bf16[2,1024,2304]{2,1,0:T(8,128)(2,1)S(1)}, bf16[2,2,2,2304,2...) custom-call(bf16[1024,2304]{1,0:T(8,128)(2,1)} %x.1, f32[2304]{0:T(1024)} %gain.1, ...), custom_call_target="tpu_custom_call" | custom-call | tf_op jit(solution)/shard_map/pallas_call | solution.py:446
  95.0 3.3 %shard_map.77 = (bf16[8192,256]{1,0:T(8,128)(2,1)}, bf16[8192,256]{1,0:T(8,128)(2,1)}, bf16[8192,256]{1,0:T(8,128)(2,1)}, f32[8,128]{1,0:T(8,128)S(1)}) custom-call(bf16[8192,256]{1,0:T(8,128)(2,1)S(1)} %get-tuple-element.20.oq.oq_in, bf16[2,8192,256]{2,1,0:T(8,128)(2,1)S(1)} %get-tuple-element.21.okv.okv_in), custom_call_target="tpu_custom_call" | custom-call | tf_op jit(solution)/shard_map/pallas_call | solution.py:470
  98.4 26.3 %shard_map.78 = (bf16[8192,256]{1,0:T(8,128)(2,1)S(1)}, bf16[2,8192,256]{2,1,0:T(8,128)(2,1)S(1)}, bf16[2,1024,2304]{2,1,0:T(8,128)(2,1)S(1)}, bf16[2,1024,256]{2,1,0:T(8,128)(2,1)S(1)}) custom-call(bf16[2,2,2,2304,256]{4,3,2,1,0:T(8,128)(2,1)S(1)} %get-tuple-element.18.w, ...), custom_call_target="tpu_custom_call", output_to_operand_aliasing={{0}: (3, {}), {1}: (4, {}), {2}: (5, {}), {3}: (6, {})} | custom-call | tf_op jit(solution)/shard_map/pallas_call | solution.py:478
  124.7 2.1 %shard_map.79 = (bf16[8192,256]{1,0:T(8,128)(2,1)}, bf16[8192,256]{1,0:T(8,128)(2,1)}, bf16[8192,256]{1,0:T(8,128)(2,1)}) custom-call(bf16[8192,256]{1,0:T(8,128)(2,1)S(1)} %get-tuple-element.25.oq, bf16[2,8192,256]{2,1,0:T(8,128)(2,1)S(1)} %get-tuple-element.26.okv, ...), custom_call_target="tpu_custom_call", output_to_operand_aliasing={{0}: (2, {}), {1}: (3, {}), {2}: (4, {})} | custom-call | tf_op jit(solution)/shard_map/pallas_call | solution.py:495

commit v14 on v12

--- a/solution.py
+++ b/solution.py
@@ -12,7 +12,9 @@
 NORM_ROWS = 32
 CHUNK = 128
 EARLY = 5
-EARLY_SENDS = 5
+SEND_ROWS = 64
+EARLY_SENDS = 10
+MORE_SENDS = 5
 OWN_ROWS = 256
 W_BLOCKS = 2
 W_FIRST = 256
@@ -36,7 +38,7 @@
         self.weight_peer = self.weight_core(self.core)
         self.group_peer = {"dp": group + 1 - 2 * self.half}
         self.follows = lax.div(2 * self.chip, chips) + self.half
-        self.sends = EARLY_SENDS + 2 * self.core
+        self.sends = EARLY_SENDS + MORE_SENDS * self.core
 
     def weight_core(self, c):
         return {"tp": 2 * self.weight_chip + c}
@@ -63,6 +65,14 @@
 
 def chunk_of(j):
     return pl.ds(pl.multiple_of(j * CHUNK, CHUNK), CHUNK)
+
+
+def sends_of(j):
+    return [j * (CHUNK // SEND_ROWS) + i for i in range(CHUNK // SEND_ROWS)]
+
+
+def send_of(u):
+    return pl.ds(pl.multiple_of(u * SEND_ROWS, SEND_ROWS), SEND_ROWS)
 
 
 def greet(barrier, peers):
@@ -172,8 +182,8 @@
     gain_load.wait()
     gain_row[...] = gain_copy[...].reshape(1, depth)
 
-    def send_n(j):
-        return remote(n.at[0, chunk_of(j)], n.at[1, chunk_of(j)], n_s, n_r.at[j], token_peer)
+    def send_n(u):
+        return remote(n.at[0, send_of(u)], n.at[1, send_of(u)], n_s, n_r.at[u], token_peer)
 
     @pl.loop(0, chunks)
     def _(j):
@@ -190,9 +200,10 @@
         def _():
             pl.semaphore_wait(barrier, 2 - follows)
 
-        @pl.when(j < sends)
-        def _():
-            send_n(j).start()
+        for u in sends_of(j):
+            @pl.when(u < sends)
+            def _():
+                send_n(u).start()
 
     own = me.block(core, me.chip)
     near = me.block(core, me.token_chip)
@@ -263,7 +274,8 @@
 
     @pl.loop(0, EARLY)
     def _(j):
-        send_n(j).wait_recv()
+        for u in sends_of(j):
+            send_n(u).wait_recv()
         start = pl.multiple_of(j * CHUNK, CHUNK)
         stage = pl.ds(pl.multiple_of(rows + start, CHUNK), CHUNK)
         at = chunk_of(j)
@@ -287,14 +299,14 @@
         arrive(okv.at[:, theirs], lkv_r.at[i], partner)
         sent(slq.at[mine], lq_s.at[i], partner)
         sent(okv.at[:, mine], lkv_s.at[i], partner)
-    @pl.loop(EARLY, sends)
-    def _(j):
-        send_n(j).wait_recv()
+    @pl.loop(EARLY_SENDS, sends)
+    def _(u):
+        send_n(u).wait_recv()
 
     for i in range(2):
         @pl.when(core == i)
         def _():
-            sent(n.at[0, pl.ds(0, (EARLY_SENDS + 2 * i) * CHUNK)], n_s, token_peer)
+            sent(n.at[0, pl.ds(0, (EARLY_SENDS + MORE_SENDS * i) * SEND_ROWS)], n_s, token_peer)
     sent(own_w, wl_s, partner)
     sent(w.at[1, 0, 0], wx_s, weight_peer)
     sent(w.at[1, 0, 0], wg_s, group_peer)
@@ -327,12 +339,12 @@
     pl.semaphore_wait(barrier, 2 + 2 * core)
     greet(barrier, (partner, me.weight_core(other_core)))
 
-    def send_n(j):
-        return remote(n.at[0, chunk_of(j)], n.at[1, chunk_of(j)], n_s, n_r.at[j], me.token_peer)
-
-    @pl.loop(me.sends, chunks)
-    def _(j):
-        send_n(j).start()
+    def send_n(u):
+        return remote(n.at[0, send_of(u)], n.at[1, send_of(u)], n_s, n_r.at[u], me.token_peer)
+
+    @pl.loop(me.sends, rows // SEND_ROWS)
+    def _(u):
+        send_n(u).start()
 
     @pl.when(core == 0)
     def _():
@@ -343,9 +355,10 @@
 
     @pl.loop(EARLY, chunks)
     def _(j):
-        @pl.when(j >= me.sends)
-        def _():
-            send_n(j).wait_recv()
+        for u in sends_of(j):
+            @pl.when(u >= me.sends)
+            def _():
+                send_n(u).wait_recv()
 
         start = pl.multiple_of(j * CHUNK, CHUNK)
         at = pl.ds(start, CHUNK)
@@ -373,7 +386,8 @@
     for i in range(2):
         @pl.when(core == i)
         def _():
-            sent(n.at[0, pl.ds((EARLY_SENDS + 2 * i) * CHUNK, rows - (EARLY_SENDS + 2 * i) * CHUNK)], n_s, me.token_peer)
+            gone = (EARLY_SENDS + MORE_SENDS * i) * SEND_ROWS
+            sent(n.at[0, pl.ds(gone, rows - gone)], n_s, me.token_peer)
 
     @pl.loop(EARLY, chunks)
     def _(j):
@@ -456,7 +470,7 @@
                 dma, dma((2, W_BLOCKS)),
                 dma, dma,
                 dma((2,)), dma((2,)),
-                dma, dma((chunks,)),
+                dma, dma((rows // SEND_ROWS,)),
                 dma, dma((2,)), dma, dma,
                 dma((2,)), dma((2,)), dma((2,)), dma((2,)),
                 dma, dma, dma, dma, dma, dma,
@@ -481,7 +495,7 @@
             scratch_shapes=[
                 pltpu.VMEM((2, rows, head), dtype),
                 pltpu.VMEM((rows - early, head), dtype),
-                dma, dma((chunks,)),
+                dma, dma((rows // SEND_ROWS,)),
                 dma, dma, dma, dma, dma, dma,
                 dma, dma((2,)), dma, dma((chunks - EARLY,)),
                 dma, dma, dma, dma,

time: 124 us -> 124 us (level)
    pallas_call x1, Pallas kernels: 85.2 us -> 87.8 us  [local_step(): pl.pallas_call(functools.partial(first_exchange, chips), out_shape=(oq_ty...]
    pallas_call x1, Pallas kernels: 32.8 us -> 30.4 us  [local_step(): pl.pallas_call(functools.partial(second_exchange, chips), out_shape=(oq_t...]
where the time goes in v14:
time: 124 us
  Pallas kernels  124 us (100%)
    pallas_call x1, Pallas kernels, local_step(): pl.pallas_call(functools.partial(first_exchange, chips), out_shape=(oq_ty...  87.8 us
    pallas_call x1, Pallas kernels, local_step(): pl.pallas_call(functools.partial(second_exchange, chips), out_shape=(oq_t...  30.4 us
    pallas_call x1, Pallas kernels, local_step(): pl.pallas_call(functools.partial(first_write, chips, rows), out_shape=(ou...  3.34 us

profile of v14, /device:TPU:113, one launch (start us, length us, event | category | flops | bytes accessed | tf_op | source)
XLA Modules:
  0.0 124.3 jit_solution(16867392065943796234)
XLA Ops:
  0.6 87.8 %shard_map.76 = (bf16[8192,256]{1,0:T(8,128)(2,1)S(1)}, bf16[2,8192,256]{2,1,0:T(8,128)(2,1)S(1)}, bf16[2,1024,2304]{2,1,0:T(8,128)(2,1)S(1)}, bf16[2,2,2,2304,2...) custom-call(bf16[1024,2304]{1,0:T(8,128)(2,1)} %x.1, f32[2304]{0:T(1024)} %gain.1, ...), custom_call_target="tpu_custom_call" | custom-call | tf_op jit(solution)/shard_map/pallas_call | solution.py:457
  88.4 3.3 %shard_map.77 = (bf16[8192,256]{1,0:T(8,128)(2,1)}, bf16[8192,256]{1,0:T(8,128)(2,1)}, bf16[8192,256]{1,0:T(8,128)(2,1)}, f32[8,128]{1,0:T(8,128)S(1)}) custom-call(bf16[8192,256]{1,0:T(8,128)(2,1)S(1)} %get-tuple-element.20.oq.oq_in, bf16[2,8192,256]{2,1,0:T(8,128)(2,1)S(1)} %get-tuple-element.21.okv.okv_in), custom_call_target="tpu_custom_call" | custom-call | tf_op jit(solution)/shard_map/pallas_call | solution.py:481
  91.8 30.4 %shard_map.78 = (bf16[8192,256]{1,0:T(8,128)(2,1)S(1)}, bf16[2,8192,256]{2,1,0:T(8,128)(2,1)S(1)}, bf16[2,1024,2304]{2,1,0:T(8,128)(2,1)S(1)}, bf16[2,1024,256]{2,1,0:T(8,128)(2,1)S(1)}) custom-call(bf16[2,2,2,2304,256]{4,3,2,1,0:T(8,128)(2,1)S(1)} %get-tuple-element.18.w, ...), custom_call_target="tpu_custom_call", output_to_operand_aliasing={{0}: (3, {}), {1}: (4, {}), {2}: (5, {}), {3}: (6, {})} | custom-call | tf_op jit(solution)/shard_map/pallas_call | solution.py:489
  122.2 2.1 %shard_map.79 = (bf16[8192,256]{1,0:T(8,128)(2,1)}, bf16[8192,256]{1,0:T(8,128)(2,1)}, bf16[8192,256]{1,0:T(8,128)(2,1)}) custom-call(bf16[8192,256]{1,0:T(8,128)(2,1)S(1)} %get-tuple-element.25.oq, bf16[2,8192,256]{2,1,0:T(8,128)(2,1)S(1)} %get-tuple-element.26.okv, ...), custom_call_target="tpu_custom_call", output_to_operand_aliasing={{0}: (2, {}), {1}: (3, {}), {2}: (4, {})} | custom-call | tf_op jit(solution)/shard_map/pallas_call | solution.py:506
